TPU v7x, 32 devices: a whole 2x2x4 slice. The times are simulated.
32 devices in a mesh: dp: 4 (over y, x), tensor: 8 (over z, core).
Axes of the slice: x: 2, y: 2, z: 4, core: 2. Of those that a mesh axis runs over, the one named last changes fastest.
Arguments:
- queries: bfloat16 [1536, 8192], P('dp', 'tensor'), may hold values from -180 to 180
- keys: bfloat16 [1536, 1024], P('dp'), may hold values from -4.5 to 4.5
- values: bfloat16 [1536, 1024], P('dp'), may hold values from -6 to 6
- grad_out: bfloat16 [1536, 8192], P('dp', 'tensor'), may hold values from -3 to 3
- weight: float32 [8192, 8192], P('dp', 'tensor'), as said below
- first_code: bfloat16 [8192, 8192], P('dp', 'tensor'), may hold values from -1 to 1, as said below
- first_rows: float32 [8192], P('dp'), may hold values from 0.2 to 5
- first_cols: float32 [8192], P('tensor'), may hold values from 0.2 to 5
- second_code: bfloat16 [8192, 8192], P('dp', 'tensor'), may hold values from 0 to 1, as said below
- second_rows: float32 [8192], P('dp'), may hold values from 0.5 to 20
- second_cols: float32 [8192], P('tensor'), may hold values from 0.5 to 20
Outputs:
- grad_queries: bfloat16 [1536, 8192], P('dp', 'tensor')
- new_weight: float32 [8192, 8192], P('dp', 'tensor')
- next_first_code: bfloat16 [8192, 8192], P('dp', 'tensor')
- next_first_rows: float32 [8192], P('dp')
- next_first_cols: float32 [8192], P('tensor')
- next_second_code: bfloat16 [8192, 8192], P('dp', 'tensor')
- next_second_rows: float32 [8192], P('dp')
- next_second_cols: float32 [8192], P('tensor')
Inputs may be any that keep to these rules, and one draw needn't show every extreme that they name: `weight`: rows 8192 onward are zero. `first_code`: rows 8192 onward are zero. `second_code`: rows 8192 onward are zero; all other entries are 0.05 or more.
All inputs are finite; a program needn't handle non-finite values.
Results may differ from a plain program's by a relative error of at most 0.023.
Values may be sent and summed in bfloat16 or wider, within the bound.
A program may use at most 128 MiB of HBM per device.

v0:
```python
import functools

import jax
import jax.numpy as jnp
from jax import lax
from jax.experimental import pallas as pl
from jax.experimental.pallas import tpu as pltpu
from jax.sharding import PartitionSpec as P

H = 64
KVH = 8
HD = 128


beta_first = 0.9
beta_second = 0.95
learning = 0.01
decay_rate = 0.1
adam_eps = 1e-08
code_eps = 1e-06
correct_first = 1.0 - 0.9**10
correct_second = 1.0 - 0.95**10


def attend(queries, key_sel, value_sel, heads_dev):
    length = queries.shape[0]
    query_heads = queries.reshape(length, heads_dev, HD)
    scores = jnp.einsum(
        "qhd,kd->hqk", query_heads, key_sel, preferred_element_type=jnp.float32
    ) * HD ** (-0.5)
    future = lax.broadcasted_iota(jnp.int32, (length, length), 1) > lax.broadcasted_iota(
        jnp.int32, (length, length), 0
    )
    scores = jnp.where(future[None], -1e30, scores)
    highest = jnp.max(scores, axis=-1, keepdims=True)
    exponent = jnp.exp(scores - highest)
    probabilities = exponent / jnp.sum(exponent, axis=-1, keepdims=True)
    weights_half = probabilities.astype(jnp.bfloat16)
    attended = jnp.einsum(
        "hqk,kd->qhd", weights_half, value_sel, preferred_element_type=jnp.float32
    )
    return (probabilities, attended.astype(jnp.bfloat16).reshape(length, heads_dev * HD))


def attend_back(probabilities, attended, grad_half, key_sel, value_sel, heads_dev):
    length = grad_half.shape[0]
    grad_heads = grad_half.reshape(length, heads_dev, HD)
    grad_probs = jnp.einsum(
        "qhd,kd->hqk", grad_heads, value_sel, preferred_element_type=jnp.float32
    )
    row_dot = jnp.sum(
        grad_heads.astype(jnp.float32)
        * attended.reshape(length, heads_dev, HD).astype(jnp.float32),
        axis=-1,
    )
    grad_scores = (probabilities * (grad_probs - row_dot.T[:, :, None])).astype(jnp.bfloat16)
    grad_query = jnp.einsum(
        "hqk,kd->qhd", grad_scores, key_sel, preferred_element_type=jnp.float32
    ) * HD ** (-0.5)
    return grad_query.astype(jnp.bfloat16).reshape(length, heads_dev * HD)


CORES = 2
CHUNKS = 4


def exchange_kernel(
    nd, nz, grad_ref, att_ref, g_ref, a_ref, zbuf,
    up_send, down_send, z_recv, own_send, d_send, d_recv, p_send, p_recv, a_send, a_recv, local_sem,
):
    d = lax.axis_index("dp")
    t = lax.axis_index("tensor")
    z = t // CORES
    c = t % CORES
    partner = t + 1 - 2 * c
    rows = grad_ref.shape[0] // CHUNKS
    has_up = z < nz - 1
    has_down = z > 0
    barrier = pltpu.get_barrier_semaphore()

    def greet(**where):
        pl.semaphore_signal(barrier, inc=1, device_id=where)

    greet(tensor=partner)
    for o in range(1, nd):
        greet(dp=(d + o) % nd)

    for o in range(1, nz):
        greet(tensor=(t + CORES * o) % (CORES * nz))
    pl.semaphore_wait(barrier, nd + nz - 1)

    def part(ch):
        return pl.ds(ch * rows, rows)

    def block(zp, ch, own):
        return grad_ref.at[part(ch)] if own else zbuf.at[zp, part(ch)]

    def up(zp, ch, own):
        return pltpu.make_async_remote_copy(
            block(zp, ch, own), zbuf.at[zp, part(ch)], up_send.at[zp, ch], z_recv.at[zp, ch],
            device_id={"tensor": t + CORES},
        )

    def down(zp, ch, own):
        return pltpu.make_async_remote_copy(
            block(zp, ch, own), zbuf.at[zp, part(ch)], down_send.at[zp, ch], z_recv.at[zp, ch],
            device_id={"tensor": t - CORES},
        )

    def to_owner(zp, ch, own):
        return pltpu.make_async_remote_copy(
            block(zp, ch, own), g_ref.at[d, c, part(ch)], d_send.at[zp, ch], d_recv.at[d, ch],
            device_id={"dp": zp},
        )

    def keep(zp, ch, own):
        return pltpu.make_async_copy(
            block(zp, ch, own), g_ref.at[d, c, part(ch)], local_sem.at[ch]
        )

    def keep_partner(zp, ch, own):
        return pltpu.make_async_remote_copy(
            block(zp, ch, own), g_ref.at[d, c, part(ch)], own_send.at[ch], p_recv.at[d, ch],
            device_id={"tensor": partner},
        )

    def to_partner(dp, ch):
        return pltpu.make_async_remote_copy(
            g_ref.at[dp, c, part(ch)], g_ref.at[dp, c, part(ch)], p_send.at[dp, ch],
            p_recv.at[dp, ch], device_id={"tensor": partner},
        )

    def att_copy(o):
        return pltpu.make_async_remote_copy(
            att_ref, a_ref.at[d], a_send.at[o], a_recv.at[o], device_id={"dp": (d + o) % nd}
        )

    def spread(zp, ch, own, act):
        @pl.when(zp == d)
        def _():
            act(keep_partner(zp, ch, own), True)
            act(keep(zp, ch, own), False)

        @pl.when(zp != d)
        def _():
            act(to_owner(zp, ch, own), True)

    def start(copy, remote):
        copy.start()

    def finish(copy, remote):
        if remote:
            copy.wait_send()
        else:
            copy.wait()

    for ch in range(CHUNKS):

        @pl.when(has_up)
        def _():
            up(z, ch, True).start()

        @pl.when(has_down)
        def _():
            down(z, ch, True).start()

        spread(z, ch, True, start)
    for o in range(1, nd):
        att_copy(o).start()
    own_att = pltpu.make_async_copy(att_ref, a_ref.at[d], local_sem.at[CHUNKS])
    own_att.start()

    for dist in range(1, nz):
        for ch in range(CHUNKS):

            @pl.when(z - dist >= 0)
            def _():
                zp = z - dist
                down(zp, ch, False).wait_recv()

                @pl.when(has_up)
                def _():
                    up(zp, ch, False).start()

                spread(zp, ch, False, start)

            @pl.when(z + dist < nz)
            def _():
                zp = z + dist
                down(zp, ch, False).wait_recv()

                @pl.when(has_down)
                def _():
                    down(zp, ch, False).start()

                spread(zp, ch, False, start)

    for ch in range(CHUNKS):
        for o in range(1, nd):
            src = (d + o) % nd
            pltpu.make_async_remote_copy(
                g_ref.at[src, c, part(ch)], g_ref.at[src, c, part(ch)], p_send.at[src, ch],
                d_recv.at[src, ch], device_id={"tensor": partner},
            ).wait_recv()
            to_partner(src, ch).start()

    own_att.wait()
    for o in range(1, nd):
        att_copy(o).wait_send()
        pltpu.make_async_remote_copy(
            att_ref, a_ref.at[(d + nd - o) % nd], a_send.at[o], a_recv.at[o],
            device_id={"dp": (d + o) % nd},
        ).wait_recv()
    for ch in range(CHUNKS):
        for src in range(nd):
            pltpu.make_async_remote_copy(
                g_ref.at[src, 1 - c, part(ch)], g_ref.at[src, 1 - c, part(ch)],
                p_send.at[src, ch], p_recv.at[src, ch], device_id={"tensor": partner},
            ).wait_recv()
        for o in range(1, nd):
            to_partner((d + o) % nd, ch).wait_send()

        @pl.when(has_up)
        def _():
            up(z, ch, True).wait_send()

        @pl.when(has_down)
        def _():
            down(z, ch, True).wait_send()

        spread(z, ch, True, finish)
        for dist in range(1, nz):

            @pl.when(z - dist >= 0)
            def _():
                @pl.when(has_up)
                def _():
                    up(z - dist, ch, False).wait_send()

                spread(z - dist, ch, False, finish)

            @pl.when(z + dist < nz)
            def _():
                @pl.when(has_down)
                def _():
                    down(z + dist, ch, False).wait_send()

                spread(z + dist, ch, False, finish)


def exchange(grad_out, attended, nd, nz):
    length, feats = grad_out.shape
    dma = pltpu.SemaphoreType.DMA
    return pl.pallas_call(
        functools.partial(exchange_kernel, nd, nz),
        out_shape=(
            jax.ShapeDtypeStruct((nd, CORES, length, feats), grad_out.dtype),
            jax.ShapeDtypeStruct((nd,) + attended.shape, attended.dtype),
        ),
        in_specs=[pl.BlockSpec(memory_space=pltpu.VMEM)] * 2,
        out_specs=(pl.BlockSpec(memory_space=pl.ANY),) * 2,
        scratch_shapes=[
            pltpu.VMEM((nz, length, feats), grad_out.dtype),
            dma((nz, CHUNKS)),
            dma((nz, CHUNKS)),
            dma((nz, CHUNKS)),
            dma((CHUNKS,)),
            dma((nz, CHUNKS)),
            dma((nd, CHUNKS)),
            dma((nd, CHUNKS)),
            dma((nd, CHUNKS)),
            dma((nd,)),
            dma((nd,)),
            dma((CHUNKS + 1,)),
        ],
        compiler_params=pltpu.CompilerParams(collective_id=0, has_side_effects=True),
    )(grad_out, attended)


def maxima_kernel(nd, nt, r_ref, c_ref, ro_ref, co_ref, rbuf, cbuf, rs, rr, cs, cr):
    d = lax.axis_index("dp")
    t = lax.axis_index("tensor")
    barrier = pltpu.get_barrier_semaphore()
    for o in range(1, nt):
        pl.semaphore_signal(barrier, inc=1, device_id={"tensor": (t + o) % nt})
    for o in range(1, nd):
        pl.semaphore_signal(barrier, inc=1, device_id={"dp": (d + o) % nd})
    pl.semaphore_wait(barrier, nt + nd - 2)
    copies = [
        pltpu.make_async_remote_copy(
            r_ref, rbuf.at[o], rs.at[o], rr.at[o], device_id={"tensor": (t + o) % nt}
        )
        for o in range(1, nt)
    ] + [
        pltpu.make_async_remote_copy(
            c_ref, cbuf.at[o], cs.at[o], cr.at[o], device_id={"dp": (d + o) % nd}
        )
        for o in range(1, nd)
    ]
    for copy in copies:
        copy.start()
    for copy in copies:
        copy.wait()
    rows = r_ref[...]
    for o in range(1, nt):
        rows = jnp.maximum(rows, rbuf[o])
    ro_ref[...] = rows
    cols = c_ref[...]
    for o in range(1, nd):
        cols = jnp.maximum(cols, cbuf[o])
    co_ref[...] = cols


def maxima(rows, cols, nd, nt):
    dma = pltpu.SemaphoreType.DMA
    vmem = pl.BlockSpec(memory_space=pltpu.VMEM)
    return pl.pallas_call(
        functools.partial(maxima_kernel, nd, nt),
        out_shape=(
            jax.ShapeDtypeStruct(rows.shape, rows.dtype),
            jax.ShapeDtypeStruct(cols.shape, cols.dtype),
        ),
        in_specs=[vmem] * 2,
        out_specs=(vmem,) * 2,
        scratch_shapes=[
            pltpu.VMEM((nt,) + rows.shape, rows.dtype),
            pltpu.VMEM((nd,) + cols.shape, cols.dtype),
            dma((nt,)),
            dma((nt,)),
            dma((nd,)),
            dma((nd,)),
        ],
        compiler_params=pltpu.CompilerParams(collective_id=1, has_side_effects=True),
    )(rows, cols)


def per_device(
    queries,
    keys,
    values,
    grad_out,
    weight,
    first_code,
    first_rows,
    first_cols,
    second_code,
    second_rows,
    second_cols,
):
    dp_count = lax.axis_size("dp")
    cols_dev = queries.shape[1]
    heads_dev = cols_dev // HD
    rows_dev = weight.shape[0]
    width_pad = dp_count * rows_dev
    tensor_index = lax.axis_index("tensor")
    kv_start = tensor_index * heads_dev // (H // KVH) * HD
    weight_half = weight.astype(jnp.bfloat16)
    length = queries.shape[0]
    key_sel = lax.dynamic_slice_in_dim(keys, kv_start, HD, 1)
    value_sel = lax.dynamic_slice_in_dim(values, kv_start, HD, 1)
    probabilities, attended = attend(queries, key_sel, value_sel, heads_dev)
    tensor_count, feats = lax.axis_size("tensor"), grad_out.shape[1]
    if rows_dev == CORES * feats and tensor_count == CORES * dp_count and length % 64 == 0:
        pieces = CORES
        mine, all_attended = exchange(grad_out, attended, dp_count, tensor_count // CORES)
        all_attended = all_attended.reshape(dp_count * length, cols_dev)
    else:
        pieces = 1
        flat = lax.all_gather(grad_out, "tensor", axis=1, tiled=True)
        flat = jnp.pad(flat, ((0, 0), (0, width_pad - flat.shape[1])))
        blocks = jnp.moveaxis(flat.reshape(length, dp_count, 1, rows_dev), 0, 2)
        mine = lax.all_to_all(blocks, "dp", 0, 0, tiled=True)
        all_attended = lax.all_gather(attended, "dp", axis=0, tiled=True)
    span = rows_dev // pieces
    parts = [mine[:, k].reshape(dp_count * length, span) for k in range(pieces)]
    partial = sum(
        jnp.dot(
            parts[k], weight_half[k * span : (k + 1) * span], preferred_element_type=jnp.float32
        )
        for k in range(pieces)
    )
    partial, all_attended = lax.optimization_barrier(
        (partial.astype(jnp.bfloat16), all_attended)
    )
    grad_half = lax.psum_scatter(
        partial, "dp", scatter_dimension=0, tiled=True
    )
    weight_grad = jnp.concatenate(
        [
            jnp.einsum("sc,sh->ch", parts[k], all_attended, preferred_element_type=jnp.float32)
            for k in range(pieces)
        ],
        axis=0,
    )
    grad_queries = attend_back(probabilities, attended, grad_half, key_sel, value_sel, heads_dev)
    first = first_code.astype(jnp.float32) * jnp.minimum(first_rows[:, None], first_cols[None, :])
    second = second_code.astype(jnp.float32) * jnp.minimum(
        second_rows[:, None], second_cols[None, :]
    )
    first_new = beta_first * first + (1.0 - beta_first) * weight_grad
    second_new = beta_second * second + (1.0 - beta_second) * weight_grad * weight_grad
    step_size = first_new / correct_first / (jnp.sqrt(second_new / correct_second) + adam_eps)
    new_weight = weight - learning * (step_size + decay_rate * weight)
    first_abs = jnp.abs(first_new)
    second_abs = jnp.abs(second_new)
    local_rows_max = jnp.stack([jnp.max(first_abs, axis=1), jnp.max(second_abs, axis=1)])
    local_cols_max = jnp.stack([jnp.max(first_abs, axis=0), jnp.max(second_abs, axis=0)])
    rows_mine, cols_mine = maxima(local_rows_max, local_cols_max, dp_count, tensor_count)
    next_first_code = (
        first_new / (jnp.minimum(rows_mine[0][:, None], cols_mine[0][None, :]) + code_eps)
    ).astype(jnp.bfloat16)
    next_second_code = (
        second_new / (jnp.minimum(rows_mine[1][:, None], cols_mine[1][None, :]) + code_eps)
    ).astype(jnp.bfloat16)
    return (
        grad_queries,
        new_weight,
        next_first_code,
        rows_mine[0],
        cols_mine[0],
        next_second_code,
        rows_mine[1],
        cols_mine[1],
    )


def solution(mesh):
    return jax.shard_map(
        per_device,
        mesh=mesh,
        in_specs=(
            P("dp", "tensor"),
            P("dp", None),
            P("dp", None),
            P("dp", "tensor"),
            P("dp", "tensor"),
            P("dp", "tensor"),
            P("dp"),
            P("tensor"),
            P("dp", "tensor"),
            P("dp"),
            P("tensor"),
        ),
        out_specs=(
            P("dp", "tensor"),
            P("dp", "tensor"),
            P("dp", "tensor"),
            P("dp"),
            P("tensor"),
            P("dp", "tensor"),
            P("dp"),
            P("tensor"),
        ),
        check_vma=False,
    )
```

profile of v0, /device:TPU:7, one launch (start us, length us, event | category | flops | bytes accessed | tf_op | source)
XLA Modules:
  0.0 179.3 jit_solution(8575246773048791553)
XLA Ops:
  7.2 0.0 copy-start
  7.2 0.0 reduce-scatter.2.cloned.1.call-start
  7.3 0.0 copy-start.7
  7.3 6.2 %convert_element_type.45 = bf16[2048,1024]{1,0:T(8,128)(2,1)} convert(f32[2048,1024]{1,0:T(8,128)} %param.15) | non-fusion elementwise | flops 2097152 | bytes 12582912 | tf_op jit(solution)/shard_map/convert_element_type | solution.py:357
  13.5 0.0 copy-done
  13.5 0.0 copy-done.7
  13.5 0.8 fusion.23
  14.3 1.5 fusion.46
  15.8 0.0 copy-start.17
  15.8 1.6 fusion.20
  17.5 0.5 copy-done.17
  18.0 1.2 copy.31.att_ref
  19.1 82.1 %shard_map.170 = (bf16[4,2,384,1024]{3,2,1,0:T(8,128)(2,1)}, bf16[4,384,1024]{2,1,0:T(8,128)(2,1)}) custom-call(bf16[384,1024]{1,0:T(8,128)(2,1)} %grad_ref.1, bf16[384,1024]{1,0:T(8,128)(2,1)} %copy.31.att_ref), custom_call_target="tpu_custom_call" | custom-call | tf_op jit(solution)/shard_map/pallas_call | solution.py:254
  101.3 0.0 copy-start.3
  101.3 4.2 %fusion.43 = (bf16[4,1,384,1024]{3,2,1,0:T(8,128)(2,1)S(1)}, bf16[4,1,384,1024]{3,2,1,0:T(8,128)(2,1)S(1)}) fusion(bf16[4,2,384,1024]{3,2,1,0:T(8,128)(2,1)} %get-tuple-element.14), kind=kLoop, calls=%fused_computation.53 | loop fusion | bytes 12582912 | tf_op jit(solution)/shard_map/slice | solution.py:375
  105.5 0.0 copy-start.4
  105.5 0.0 copy-start.6
  105.5 0.0 copy-done.3
  105.5 3.5 %fusion.16 = f32[1536,1024]{1,0:T(8,128)S(1)} fusion(bf16[1536,1024]{1,0:T(8,128)(2,1)S(1)} %bitcast.71, bf16[2048,1024]{1,0:T(8,128)(2,1)S(1)} %copy-done.3), kind=kOutput, calls=%fused_computation.29 | convolution fusion | flops 3221225472 | bytes 11534336 | tf_op jit(solution)/shard_map/dot_general | solution.py:377
  109.0 0.0 copy-done.4
  109.0 0.0 copy-done.6
  109.0 5.1 %add_convert_fusion = bf16[1536,1024]{1,0:T(8,128)(2,1)} fusion(f32[1536,1024]{1,0:T(8,128)S(1)} %fusion.16, bf16[1536,1024]{1,0:T(8,128)(2,1)S(1)} %bitcast.73, bf16[2048,1024]{1,0:T(8,128)(2,1)S(1)} %copy-done.3), kind=kOutput, calls=%fused_computation.12 | convolution fusion | flops 3224371200 | bytes 14680064 | tf_op jit(solution)/shard_map/dot_general | solution.py:377
  114.1 0.0 reduce-scatter.2.cloned.1.call-update
  114.1 0.0 copy-start.5
  114.2 0.0 copy-start.16
  114.2 6.6 %fusion.48 = f32[1024,1024]{1,0:T(8,128)S(1)} fusion(bf16[1536,1024]{1,0:T(8,128)(2,1)} %bitcast.74, bf16[1536,1024]{1,0:T(8,128)(2,1)} %bitcast.89), kind=kOutput, calls=%fused_computation.58 | convolution fusion | flops 3221225472 | bytes 10485760 | tf_op jit(solution)/shard_map/sc,sh->ch/dot_general | solution.py:390
  120.7 0.0 copy-done.5
  120.8 0.0 copy-done.16
  120.8 0.0 copy-start.1
  120.8 0.0 copy-start.2
  120.8 0.0 copy-start.12
  120.8 0.0 copy-start.13
  120.8 0.0 copy-start.14
  120.8 0.0 copy-start.15
  120.8 3.5 %fusion.47 = f32[1024,1024]{1,0:T(8,128)S(1)} fusion(bf16[1536,1024]{1,0:T(8,128)(2,1)S(1)} %bitcast.72, bf16[1536,1024]{1,0:T(8,128)(2,1)S(1)} %bitcast.90), kind=kOutput, calls=%fused_computation.57 | convolution fusion | flops 3221225472 | bytes 10485760 | tf_op jit(solution)/shard_map/sc,sh->ch/dot_general | solution.py:390
  124.4 0.0 copy-done.1
  124.4 0.0 copy-done.2
  124.4 0.0 copy-done.12
  124.4 0.0 copy-done.13
  124.4 0.0 copy-done.14
  124.4 0.0 copy-done.15
  124.4 10.8 %abs_reduce_fusion.2 = (f32[1024]{0:T(1024)S(1)}, f32[2048]{0:T(1024)S(1)}, f32[2048,1024]{1,0:T(8,128)}, f32[2048]{0:T(1024)S(1)}, f32[1024]{0:T(1024)S(1)}, /*index=5*/f32[2048,1024]{1,0:T(8,128)}) fusion(f32[1024,1024]{1,0:T(8,128)S(1)} %fusion.48, f32[1024,1024]{1,0:T(8,128)S(1)} %fusion.47, f32[1024]{0:T(1024)S(1)} %copy-done.14, ...), kind=kLoop, calls=%fused_computation.10 | loop fusion | flops 41936896 | bytes 33603584 | tf_op jit(solution)/shard_map/reduce_max | solution.py:407
  135.3 0.6 pad_maximum_fusion.2.c_ref
  135.9 0.6 pad_maximum_fusion.1.r_ref
  136.5 7.1 %shard_map.171 = (f32[2,2048]{1,0:T(2,128)}, f32[2,1024]{1,0:T(2,128)}) custom-call(f32[2,2048]{1,0:T(2,128)} %pad_maximum_fusion.1.r_ref, f32[2,1024]{1,0:T(2,128)} %pad_maximum_fusion.2.c_ref), custom_call_target="tpu_custom_call" | custom-call | tf_op jit(solution)/shard_map/pallas_call | solution.py:317
  143.6 0.8 fusion.45
  144.4 0.0 copy-start.10
  144.4 0.0 copy-start.11
  144.4 0.8 fusion.44
  145.2 0.0 copy-start.8
  145.2 0.0 copy-start.9
  145.2 20.6 %divide_convert_fusion = (bf16[2048,1024]{1,0:T(8,128)(2,1)}, f32[2048,1024]{1,0:T(8,128)}, bf16[2048,1024]{1,0:T(8,128)(2,1)}) fusion(f32[2048,1024]{1,0:T(8,128)} %get-tuple-element.39, f32[1024]{0:T(1024)S(1)} %bitcast.84, f32[2048]{0:T(1024)S(1)} %bitcast.78, f32[2048,1024]{1,0:T(8,128)} %param.15, f32[2048,1024]{1,0:T(8,128)} %get-tuple-element.32, ...), kind=kLoop, calls=%fused_computation.4 | loop fusion | flops 33554432 | bytes 41967616 | tf_op jit(solution)/shard_map/convert_element_type | solution.py:414
  165.8 0.0 copy-done.10
  165.8 0.0 copy-done.11
  165.8 0.0 copy-done.8
  165.9 0.0 copy-done.9
  165.9 0.0 reduce-scatter.2.cloned.1.call-done
  165.9 1.5 copy.23
  167.4 0.2 multiply_reduce_fusion
  167.6 3.6 %multiply_convert_fusion = bf16[128,8,384]{2,0,1:T(8,128)(2,1)S(1)} fusion(bf16[384,8,128]{0,2,1:T(8,128)(2,1)S(1)} %bitcast.70, f32[8,384]{1,0:T(8,128)S(1)} %bitcast.88, f32[8,384,384]{1,2,0:T(8,128)} %copy-done.17, f32[8,384]{1,0:T(8,128)S(1)} %get-tuple-element.46, bf16[384,1024]{1,0:T(8,128)(2,1)} %param.13, s32[]{:T(128)S(6)} %select_n.14, ...), kind=kOutput, calls=%fused_computation.31 | convolution fusion | flops 609484800 | bytes 6513664 | tf_op jit(solution)/shard_map/hqk,kd->qhd/dot_general | solution.py:57
  171.2 1.2 copy.26
  (1 shorter events, 0.0 us)
Async XLA Ops:
  7.2 6.3 %copy-start = (bf16[384,1024]{1,0:T(8,128)(2,1)S(1)}, bf16[384,1024]{1,0:T(8,128)(2,1)}, u32[]{:S(2)}) copy-start(bf16[384,1024]{1,0:T(8,128)(2,1)} %param.12) | copy-start | bytes 2359300
  7.2 158.7 %reduce-scatter.2.cloned.1.call-start = ((), (), s32[]{:S(2)}) async-start(), calls=%async_computation.1 | async-start | bytes 3932160 | tf_op jit(solution)/shard_map/reduce_scatter | solution.py:385
  7.3 6.2 %copy-start.7 = (bf16[384,1024]{1,0:T(8,128)(2,1)S(1)}, bf16[384,1024]{1,0:T(8,128)(2,1)}, u32[]{:S(2)}) copy-start(bf16[384,1024]{1,0:T(8,128)(2,1)} %param.11) | copy-start | bytes 2359300
  15.8 2.1 %copy-start.17 = (f32[8,384,384]{1,2,0:T(8,128)}, f32[8,384,384]{1,2,0:T(8,128)S(1)}, u32[]{:S(2)}) copy-start(f32[8,384,384]{1,2,0:T(8,128)S(1)} %get-tuple-element.47) | copy-start | bytes 14155780
  101.3 4.3 %copy-start.3 = (bf16[2048,1024]{1,0:T(8,128)(2,1)S(1)}, bf16[2048,1024]{1,0:T(8,128)(2,1)}, u32[]{:S(2)}) copy-start(bf16[2048,1024]{1,0:T(8,128)(2,1)} %convert_element_type.45) | copy-start | bytes 12582916
  105.5 3.5 %copy-start.4 = (bf16[4,1,384,1024]{3,2,1,0:T(8,128)(2,1)}, bf16[4,1,384,1024]{3,2,1,0:T(8,128)(2,1)S(1)}, u32[]{:S(2)}) copy-start(bf16[4,1,384,1024]{3,2,1,0:T(8,128)(2,1)S(1)} %get-tuple-element.41) | copy-start | bytes 9437188
  105.5 3.5 %copy-start.6 = (bf16[4,1,384,1024]{3,2,1,0:T(8,128)(2,1)}, bf16[4,1,384,1024]{3,2,1,0:T(8,128)(2,1)S(1)}, u32[]{:S(2)}) copy-start(bf16[4,1,384,1024]{3,2,1,0:T(8,128)(2,1)S(1)} %get-tuple-element.40) | copy-start | bytes 9437188
  114.1 6.6 %copy-start.5 = (bf16[4,1,384,1024]{3,2,1,0:T(8,128)(2,1)S(1)}, bf16[4,1,384,1024]{3,2,1,0:T(8,128)(2,1)}, u32[]{:S(2)}) copy-start(bf16[4,1,384,1024]{3,2,1,0:T(8,128)(2,1)} %copy-done.4) | copy-start | bytes 9437188
  114.2 6.6 %copy-start.16 = (bf16[4,384,1024]{2,1,0:T(8,128)(2,1)S(1)}, bf16[4,384,1024]{2,1,0:T(8,128)(2,1)}, u32[]{:S(2)}) copy-start(bf16[4,384,1024]{2,1,0:T(8,128)(2,1)} %get-tuple-element.15) | copy-start | bytes 9437188
  120.8 3.6 %copy-start.1 = (bf16[2048,1024]{1,0:T(8,128)(2,1)S(1)}, bf16[2048,1024]{1,0:T(8,128)(2,1)}, u32[]{:S(2)}) copy-start(bf16[2048,1024]{1,0:T(8,128)(2,1)} %param.16) | copy-start | bytes 12582916
  120.8 3.6 %copy-start.2 = (bf16[2048,1024]{1,0:T(8,128)(2,1)S(1)}, bf16[2048,1024]{1,0:T(8,128)(2,1)}, u32[]{:S(2)}) copy-start(bf16[2048,1024]{1,0:T(8,128)(2,1)} %param.19) | copy-start | bytes 12582916
  120.8 3.6 %copy-start.12 = (f32[2048]{0:T(1024)S(1)}, f32[2048]{0:T(1024)}, u32[]{:S(2)}) copy-start(f32[2048]{0:T(1024)} %param.17) | copy-start | bytes 24580
  120.8 3.6 %copy-start.13 = (f32[2048]{0:T(1024)S(1)}, f32[2048]{0:T(1024)}, u32[]{:S(2)}) copy-start(f32[2048]{0:T(1024)} %param.20) | copy-start | bytes 24580
  120.8 3.6 %copy-start.14 = (f32[1024]{0:T(1024)S(1)}, f32[1024]{0:T(1024)}, u32[]{:S(2)}) copy-start(f32[1024]{0:T(1024)} %param.18) | copy-start | bytes 12292
  120.8 3.6 %copy-start.15 = (f32[1024]{0:T(1024)S(1)}, f32[1024]{0:T(1024)}, u32[]{:S(2)}) copy-start(f32[1024]{0:T(1024)} %param.21) | copy-start | bytes 12292
  144.4 21.5 %copy-start.10 = (f32[1,1024]{1,0:T(1,128)}, f32[1,1024]{1,0:T(1,128)S(1)}, u32[]{:S(2)}) copy-start(f32[1,1024]{1,0:T(1,128)S(1)} %get-tuple-element.44) | copy-start | bytes 12292
  144.4 21.5 %copy-start.11 = (f32[1,1024]{1,0:T(1,128)}, f32[1,1024]{1,0:T(1,128)S(1)}, u32[]{:S(2)}) copy-start(f32[1,1024]{1,0:T(1,128)S(1)} %get-tuple-element.45) | copy-start | bytes 12292
  145.2 20.6 %copy-start.8 = (f32[1,2048]{1,0:T(1,128)}, f32[1,2048]{1,0:T(1,128)S(1)}, u32[]{:S(2)}) copy-start(f32[1,2048]{1,0:T(1,128)S(1)} %get-tuple-element.42) | copy-start | bytes 24580
  145.2 20.6 %copy-start.9 = (f32[1,2048]{1,0:T(1,128)}, f32[1,2048]{1,0:T(1,128)S(1)}, u32[]{:S(2)}) copy-start(f32[1,2048]{1,0:T(1,128)S(1)} %get-tuple-element.43) | copy-start | bytes 24580
Sparse Core Ops, SparseCore 0:
  114.3 41.4 reduce-scatter.1
where the time goes:
time: 181 us; the launch traced here: 179 us
  Pallas kernels  89.2 us (49%)
  other arithmetic  40.6 us (22%)
  matrix products  24.7 us (14%)
  between operations  14.4 us (8%)
  local copies, waits for them, and re-layouts  10.2 us (6%)
    pallas_call x1, Pallas kernels, exchange(): pl.pallas_call(functools.partial(exchange_kernel, nd, nz), out_shape=(jax...  82.1 us
    convert_element_type x1, other arithmetic, per_device(): next_second_code = (second_new / (jnp.minimum(rows_mine[1][:, None], cols...  20.6 us
    reduce_max x1, other arithmetic, per_device(): jnp.max(first_abs, axis=0)  10.8 us
    dot_general x2, matrix products, per_device(): jnp.einsum('sc,sh->ch', parts[k], all_attended, preferred_element_type=jn...  10.1 us
    dot_general x2, matrix products, per_device(): jnp.dot(parts[k], weight_half[k * span:(k + 1) * span], preferred_element...  8.57 us
    pallas_call x1, Pallas kernels, maxima(): pl.pallas_call(functools.partial(maxima_kernel, nd, nt), out_shape=(jax.S...  7.08 us
    convert_element_type x1, other arithmetic, per_device(): weight_half = weight.astype(jnp.bfloat16)  6.16 us
    slice x1, local copies, waits for them, and re-layouts, per_device(): parts = [mine[:, k].reshape(dp_count * length, span) for k in range(pieces)]  4.21 us
  transfers between devices with their start and end apart: 1, of which 0 were waited for; matrix products, arithmetic and copies ran while one was open for 25% of the time, Pallas kernels for 4%

commit v1 on v0

v1 whole, which is shorter than its diff:
```python
import functools

import jax
import jax.numpy as jnp
from jax import lax
from jax.experimental import pallas as pl
from jax.experimental.pallas import tpu as pltpu
from jax.sharding import PartitionSpec as P

H = 64
KVH = 8
HD = 128


beta_first = 0.9
beta_second = 0.95
learning = 0.01
decay_rate = 0.1
adam_eps = 1e-08
code_eps = 1e-06
correct_first = 1.0 - 0.9**10
correct_second = 1.0 - 0.95**10


def attend(queries, key_sel, value_sel, heads_dev):
    length = queries.shape[0]
    query_heads = queries.reshape(length, heads_dev, HD)
    scores = jnp.einsum(
        "qhd,kd->hqk", query_heads, key_sel, preferred_element_type=jnp.float32
    ) * HD ** (-0.5)
    future = lax.broadcasted_iota(jnp.int32, (length, length), 1) > lax.broadcasted_iota(
        jnp.int32, (length, length), 0
    )
    scores = jnp.where(future[None], -1e30, scores)
    highest = jnp.max(scores, axis=-1, keepdims=True)
    exponent = jnp.exp(scores - highest)
    probabilities = exponent / jnp.sum(exponent, axis=-1, keepdims=True)
    weights_half = probabilities.astype(jnp.bfloat16)
    attended = jnp.einsum(
        "hqk,kd->qhd", weights_half, value_sel, preferred_element_type=jnp.float32
    )
    return (probabilities, attended.astype(jnp.bfloat16).reshape(length, heads_dev * HD))


def attend_back(probabilities, attended, grad_half, key_sel, value_sel, heads_dev):
    length = grad_half.shape[0]
    grad_heads = grad_half.reshape(length, heads_dev, HD)
    grad_probs = jnp.einsum(
        "qhd,kd->hqk", grad_heads, value_sel, preferred_element_type=jnp.float32
    )
    row_dot = jnp.sum(
        grad_heads.astype(jnp.float32)
        * attended.reshape(length, heads_dev, HD).astype(jnp.float32),
        axis=-1,
    )
    grad_scores = (probabilities * (grad_probs - row_dot.T[:, :, None])).astype(jnp.bfloat16)
    grad_query = jnp.einsum(
        "hqk,kd->qhd", grad_scores, key_sel, preferred_element_type=jnp.float32
    ) * HD ** (-0.5)
    return grad_query.astype(jnp.bfloat16).reshape(length, heads_dev * HD)


CORES = 2


def maxima_kernel(nd, nt, r_ref, c_ref, ro_ref, co_ref, rbuf, cbuf, rs, rr, cs, cr):
    d = lax.axis_index("dp")
    t = lax.axis_index("tensor")
    barrier = pltpu.get_barrier_semaphore()
    for o in range(1, nt):
        pl.semaphore_signal(barrier, inc=1, device_id={"tensor": (t + o) % nt})
    for o in range(1, nd):
        pl.semaphore_signal(barrier, inc=1, device_id={"dp": (d + o) % nd})
    pl.semaphore_wait(barrier, nt + nd - 2)
    copies = [
        pltpu.make_async_remote_copy(
            r_ref, rbuf.at[o], rs.at[o], rr.at[o], device_id={"tensor": (t + o) % nt}
        )
        for o in range(1, nt)
    ] + [
        pltpu.make_async_remote_copy(
            c_ref, cbuf.at[o], cs.at[o], cr.at[o], device_id={"dp": (d + o) % nd}
        )
        for o in range(1, nd)
    ]
    for copy in copies:
        copy.start()
    for copy in copies:
        copy.wait()
    rows = r_ref[...]
    for o in range(1, nt):
        rows = jnp.maximum(rows, rbuf[o])
    ro_ref[...] = rows
    cols = c_ref[...]
    for o in range(1, nd):
        cols = jnp.maximum(cols, cbuf[o])
    co_ref[...] = cols


def maxima(rows, cols, nd, nt):
    dma = pltpu.SemaphoreType.DMA
    vmem = pl.BlockSpec(memory_space=pltpu.VMEM)
    return pl.pallas_call(
        functools.partial(maxima_kernel, nd, nt),
        out_shape=(
            jax.ShapeDtypeStruct(rows.shape, rows.dtype),
            jax.ShapeDtypeStruct(cols.shape, cols.dtype),
        ),
        in_specs=[vmem] * 2,
        out_specs=(vmem,) * 2,
        scratch_shapes=[
            pltpu.VMEM((nt,) + rows.shape, rows.dtype),
            pltpu.VMEM((nd,) + cols.shape, cols.dtype),
            dma((nt,)),
            dma((nt,)),
            dma((nd,)),
            dma((nd,)),
        ],
        compiler_params=pltpu.CompilerParams(collective_id=1, has_side_effects=True),
    )(rows, cols)


PARTS = 3
HALVES = 2


def halves(width):
    return [pl.ds(k * (width // HALVES), width // HALVES) for k in range(HALVES)]


def fused_kernel(
    nd, nz,
    q_ref, k_ref, v_ref, grad_ref, w_hbm, fc_hbm, sc_hbm, fr_ref, fcol_ref, sr_ref, scol_ref,
    gq_ref, fn_hbm, sn_hbm, rmax_ref, cmax_ref,
    zbuf, g, gt, a, wh, stage, partial, r1, r2, mid, prob, fcv, scv, rb1, rb2,
    rloc, cloc, cacc, rbuf, cbuf, kv_k, kv_v,
    up_send, down_send, z_recv, own_send, d_send, d_recv, p_send, p_recv,
    a_send, a_recv, f_send, s1_send, s1_recv, s2_send, s2_recv,
    w_sem, c_sem, o_sem, rs, rr, cs, cr,
):
    d = lax.axis_index("dp")
    t = lax.axis_index("tensor")
    z = t // CORES
    c = t % CORES
    partner = t + 1 - 2 * c
    xn = d + 1 - 2 * (d % 2)
    yn = (d + 2) % 4
    dg = 3 - d
    length, width = grad_ref.shape
    rows = length // PARTS
    heads = width // HD
    total = w_hbm.shape[0]
    nt = CORES * nz
    has_up = z < nz - 1
    has_down = z > 0
    tile = stage.shape[1]
    tiles = total // tile
    far = jnp.abs(z - d)
    alpha, beta = halves(width)
    chunks = range(PARTS)
    scale = HD ** (-0.5)

    fetch_w = [
        pltpu.make_async_copy(w_hbm.at[pl.ds(i * tile, tile)], stage.at[i % 2], w_sem.at[i % 2])
        for i in range(tiles)
    ]
    fetch_c = [
        pltpu.make_async_copy(fc_hbm, fcv, c_sem.at[0]),
        pltpu.make_async_copy(sc_hbm, scv, c_sem.at[1]),
    ]
    fetch_w[0].start()
    fetch_w[1].start()

    barrier = pltpu.get_barrier_semaphore()
    for o in range(1, nt):
        pl.semaphore_signal(barrier, inc=1, device_id={"tensor": (t + o) % nt})
    for o in range(1, nd):
        pl.semaphore_signal(barrier, inc=1, device_id={"dp": (d + o) % nd})
    pl.semaphore_wait(barrier, nt + nd - 2)

    def part(ch):
        return pl.ds(ch * rows, rows)

    def block(zp, ch, own):
        return grad_ref.at[part(ch)] if own else zbuf.at[zp, ch]

    def up(zp, ch, own):
        return pltpu.make_async_remote_copy(
            block(zp, ch, own), zbuf.at[zp, ch], up_send.at[zp, ch], z_recv.at[zp, ch],
            device_id={"tensor": t + CORES},
        )

    def down(zp, ch, own):
        return pltpu.make_async_remote_copy(
            block(zp, ch, own), zbuf.at[zp, ch], down_send.at[zp, ch], z_recv.at[zp, ch],
            device_id={"tensor": t - CORES},
        )

    def to_owner(zp, ch, own):
        return pltpu.make_async_remote_copy(
            block(zp, ch, own), g.at[ch, c, d], d_send.at[zp, ch], d_recv.at[d, ch],
            device_id={"dp": zp},
        )

    def keep_partner(zp, ch, own):
        return pltpu.make_async_remote_copy(
            block(zp, ch, own), g.at[ch, c, d], own_send.at[ch], p_recv.at[d, ch],
            device_id={"tensor": partner},
        )

    def to_partner(src, ch):
        return pltpu.make_async_remote_copy(
            g.at[ch, c, src], g.at[ch, c, src], p_send.at[src, ch], p_recv.at[src, ch],
            device_id={"tensor": partner},
        )

    def spread(zp, ch, own):
        @pl.when(zp == d)
        def _():
            keep_partner(zp, ch, own).start()
            g[ch, c, d] = grad_ref[part(ch)] if own else zbuf[zp, ch]

        @pl.when(zp != d)
        def _():
            to_owner(zp, ch, own).start()

    def spread_done(zp, ch, own):
        @pl.when(zp == d)
        def _():
            keep_partner(zp, ch, own).wait_send()

        @pl.when(zp != d)
        def _():
            to_owner(zp, ch, own).wait_send()

    def pass_on(ch):
        for o in range(1, nd):
            src = (d + o) % nd
            pltpu.make_async_remote_copy(
                g.at[ch, c, src], g.at[ch, c, src], p_send.at[src, ch], d_recv.at[src, ch],
                device_id={"tensor": partner},
            ).wait_recv()
            to_partner(src, ch).start()

    def att_send(way, ch):
        return pltpu.make_async_remote_copy(
            a.at[d, part(ch)], a.at[d, part(ch)], a_send.at[way, ch], a_recv.at[0, d, ch],
            device_id={"dp": (xn, yn)[way]},
        )

    def att_relay(way, ch):
        src = (xn, yn)[way]
        half = (alpha, beta)[way]
        return pltpu.make_async_remote_copy(
            a.at[src, part(ch), half], a.at[src, part(ch), half], f_send.at[way, ch],
            a_recv.at[1 + way, src, ch], device_id={"dp": (yn, xn)[way]},
        )

    def att_pass(ch):
        for way in range(2):
            src = (xn, yn)[way]
            pltpu.make_async_remote_copy(
                a.at[src, part(ch)], a.at[src, part(ch)], a_send.at[way, ch],
                a_recv.at[0, src, ch], device_id={"dp": src},
            ).wait_recv()
            att_relay(way, ch).start()

    def att_wait(ch):
        for way in range(2):
            half = (alpha, beta)[way]
            pltpu.make_async_remote_copy(
                a.at[dg, part(ch), half], a.at[dg, part(ch), half], f_send.at[way, ch],
                a_recv.at[1 + way, dg, ch], device_id={"dp": (yn, xn)[way]},
            ).wait_recv()

    def first_hop(way, which, ch):
        near = (xn, yn)[way]
        half = (alpha, beta)[way]
        dest = (near, dg)[which]
        return pltpu.make_async_remote_copy(
            partial.at[ch, dest, :, half], r1.at[ch, which, :, half], s1_send.at[way, which, ch],
            s1_recv.at[way, which, ch], device_id={"dp": near},
        )

    def second_hop(way, ch):
        half = (alpha, beta)[way]
        return pltpu.make_async_remote_copy(
            mid.at[ch, :, half], r2.at[ch, :, half], s2_send.at[way, ch], s2_recv.at[way, ch],
            device_id={"dp": (yn, xn)[way]},
        )

    def cast_weight(i):
        fetch_w[i].wait()
        wh[pl.ds(i * tile, tile)] = stage[i % 2].astype(jnp.bfloat16)
        if i + 2 < tiles:
            fetch_w[i + 2].start()

    def project(ch):
        span = 256

        def body(n, carry):
            cols = pl.ds(pl.multiple_of(n * span, span), span)
            acc = None
            for p in range(CORES):
                lhs = g[ch, p].reshape(nd * rows, width)
                term = jnp.dot(
                    lhs, wh[pl.ds(p * width, width), cols], preferred_element_type=jnp.float32
                )
                acc = term if acc is None else acc + term
            partial[ch, :, :, cols] = acc.astype(jnp.bfloat16).reshape(nd, rows, span)
            return carry

        lax.fori_loop(0, width // span, body, 0)

    def turn(ch):
        def body(s, carry):
            at = pl.ds(pl.multiple_of(s * length + ch * rows, rows), rows)
            for p in range(CORES):
                gt[pl.ds(p * width, width), at] = g[ch, p, s].T
            return carry

        lax.fori_loop(0, nd, body, 0)

    def attend_fwd():
        kv = pl.multiple_of(t * heads // (H // KVH) * HD, HD)
        kv_k[...] = k_ref[:, pl.ds(kv, HD)]
        kv_v[...] = v_ref[:, pl.ds(kv, HD)]

        def body(h, carry):
            lanes = pl.ds(pl.multiple_of(h * HD, HD), HD)
            scores = lax.dot_general(
                q_ref[:, lanes], kv_k[...], (((1,), (1,)), ((), ())),
                preferred_element_type=jnp.float32,
            ) * scale
            future = lax.broadcasted_iota(jnp.int32, (length, length), 1) > (
                lax.broadcasted_iota(jnp.int32, (length, length), 0)
            )
            scores = jnp.where(future, -1e30, scores)
            exponent = jnp.exp(scores - jnp.max(scores, axis=-1, keepdims=True))
            probs = exponent / jnp.sum(exponent, axis=-1, keepdims=True)
            prob[h] = probs
            out = jnp.dot(
                probs.astype(jnp.bfloat16), kv_v[...], preferred_element_type=jnp.float32
            )
            a[d, :, lanes] = out.astype(jnp.bfloat16)
            return carry

        lax.fori_loop(0, heads, body, 0)

    def attend_bwd(ch):
        def body(h, carry):
            lanes = pl.ds(pl.multiple_of(h * HD, HD), HD)
            grad = (
                partial[ch, d, :, lanes].astype(jnp.float32)
                + r1[ch, 0, :, lanes].astype(jnp.float32)
                + r2[ch, :, lanes].astype(jnp.float32)
            ).astype(jnp.bfloat16)
            grad_probs = lax.dot_general(
                grad, kv_v[...], (((1,), (1,)), ((), ())), preferred_element_type=jnp.float32
            )
            row_dot = jnp.sum(
                grad.astype(jnp.float32) * a[d, part(ch), lanes].astype(jnp.float32),
                axis=-1, keepdims=True,
            )
            grad_scores = (prob[h, part(ch)] * (grad_probs - row_dot)).astype(jnp.bfloat16)
            out = jnp.dot(grad_scores, kv_k[...], preferred_element_type=jnp.float32) * scale
            gq_ref[part(ch), lanes] = out.astype(jnp.bfloat16)
            return carry

        lax.fori_loop(0, heads, body, 0)

    def column(row):
        return jnp.broadcast_to(row, (HD, HD)).T

    def scales():
        for k in range(total // HD):
            rb1[pl.ds(k * HD, HD)] = column(fr_ref[pl.ds(k, 1)] * beta_first)
            rb2[pl.ds(k * HD, HD)] = column(sr_ref[pl.ds(k, 1)] * beta_second)
        cacc[...] = jnp.zeros_like(cacc)

    def moments(i):
        at = pl.ds(i * tile, tile)
        span = 256

        def body(n, carry):
            high1, high2 = carry
            start = pl.multiple_of(n * span, span)
            grad = jnp.dot(
                gt[at], a[:, :, pl.ds(start, span)].reshape(nd * length, span),
                preferred_element_type=jnp.float32,
            )
            for j in range(span // HD):
                lanes = pl.ds(pl.multiple_of(start + j * HD, HD), HD)
                dw = grad[:, j * HD : (j + 1) * HD]
                first = fcv[at, lanes].astype(jnp.float32) * jnp.minimum(
                    rb1[at], fcol_ref[:, lanes] * beta_first
                ) + (1.0 - beta_first) * dw
                second = scv[at, lanes].astype(jnp.float32) * jnp.minimum(
                    rb2[at], scol_ref[:, lanes] * beta_second
                ) + (1.0 - beta_second) * dw * dw
                fcv[at, lanes] = first.astype(jnp.bfloat16)
                scv[at, lanes] = second.astype(jnp.bfloat16)
                first, second = jnp.abs(first), jnp.abs(second)
                high1 = jnp.maximum(high1, first)
                high2 = jnp.maximum(high2, second)
                cacc[0, :, lanes] = jnp.maximum(
                    cacc[0, :, lanes], jnp.max(first.reshape(tile // 8, 8, HD), axis=0)
                )
                cacc[1, :, lanes] = jnp.maximum(
                    cacc[1, :, lanes], jnp.max(second.reshape(tile // 8, 8, HD), axis=0)
                )
            return high1, high2

        zero = jnp.zeros((tile, HD), jnp.float32)
        high = lax.fori_loop(0, width // span, body, (zero, zero))
        for m in range(2):
            for k in range(tile // HD):
                piece = high[m][k * HD : (k + 1) * HD].T
                rloc[m, pl.ds(i * (tile // HD) + k, 1)] = jnp.max(piece, axis=0, keepdims=True)

    put_out = [
        [
            pltpu.make_async_copy(
                fcv.at[pl.ds(i * tile, tile)], fn_hbm.at[pl.ds(i * tile, tile)], o_sem.at[0, i]
            ),
            pltpu.make_async_copy(
                scv.at[pl.ds(i * tile, tile)], sn_hbm.at[pl.ds(i * tile, tile)], o_sem.at[1, i]
            ),
        ]
        for i in range(tiles)
    ]
    row_copies = [
        pltpu.make_async_remote_copy(
            rloc, rbuf.at[o], rs.at[o], rr.at[o], device_id={"tensor": (t + o) % nt}
        )
        for o in range(1, nt)
    ]
    col_copies = [
        pltpu.make_async_remote_copy(
            cloc, cbuf.at[o], cs.at[o], cr.at[o], device_id={"dp": (d + o) % nd}
        )
        for o in range(1, nd)
    ]

    def reduce_first(ch):
        for which in (1, 0):
            for way in range(2):
                first_hop(way, which, ch).start()

    def reduce_mid(ch):
        for way in range(2):
            half = (alpha, beta)[way]
            first_hop(way, 1, ch).wait_recv()
            mid[ch, :, half] = (
                partial[ch, (yn, xn)[way], :, half].astype(jnp.float32)
                + r1[ch, 1, :, half].astype(jnp.float32)
            ).astype(jnp.bfloat16)

    def reduce_next(ch):
        for way in range(2):
            second_hop(way, ch).start()

    def reduce_wait(ch):
        for way in range(2):
            first_hop(way, 0, ch).wait_recv()
            second_hop(way, ch).wait_recv()

    for ch in chunks:

        @pl.when(has_up)
        def _():
            up(z, ch, True).start()

        @pl.when(has_down)
        def _():
            down(z, ch, True).start()

        spread(z, ch, True)

    fetch_c[0].start()
    fetch_c[1].start()
    attend_fwd()
    cast_weight(0)
    cast_weight(1)

    jobs = {
        0: [lambda: cast_weight(2), lambda: cast_weight(3)],
        1: [lambda: cast_weight(4), lambda: cast_weight(5)],
        2: [lambda: cast_weight(6), lambda: cast_weight(7)],
        3: [scales],
    }
    step = 0
    for dist in range(1, nz):
        for ch in chunks:

            @pl.when(z - dist >= 0)
            def _():
                zp = z - dist
                down(zp, ch, False).wait_recv()

                @pl.when(has_up)
                def _():
                    up(zp, ch, False).start()

                spread(zp, ch, False)

            @pl.when(z + dist < nz)
            def _():
                zp = z + dist
                down(zp, ch, False).wait_recv()

                @pl.when(has_down)
                def _():
                    down(zp, ch, False).start()

                spread(zp, ch, False)

            if dist == 1:
                att_send(0, ch).start()
                att_send(1, ch).start()

            @pl.when(far == dist - 1)
            def _():
                pass_on(ch)

            if dist == 3:
                att_pass(ch)
            for job in jobs.get(step, []):
                job()
            step += 1
    last = nz - 1

    def gathered(ch):
        @pl.when(far == last)
        def _():
            pass_on(ch)

        for src in range(nd):
            pltpu.make_async_remote_copy(
                g.at[ch, 1 - c, src], g.at[ch, 1 - c, src], p_send.at[src, ch],
                p_recv.at[src, ch], device_id={"tensor": partner},
            ).wait_recv()

    for ch in chunks:
        gathered(ch)
        project(ch)
        turn(ch)
        reduce_first(ch)
    for copy in fetch_c:
        copy.wait()
    for ch in chunks:
        att_wait(ch)
    after = {2: lambda: reduce_mid(0), 3: lambda: reduce_next(0), 4: lambda: reduce_mid(1),
             5: lambda: reduce_next(1), 6: lambda: reduce_mid(2), 7: lambda: reduce_next(2)}
    for i in range(tiles):
        moments(i)
        if i in after:
            after[i]()
        if i:
            put_out[i - 1][0].start()
            put_out[i - 1][1].start()
    for m in range(2):
        cloc[pl.ds(m, 1)] = jnp.max(cacc[m], axis=0, keepdims=True)
    put_out[tiles - 1][0].start()
    put_out[tiles - 1][1].start()
    for copy in row_copies + col_copies:
        copy.start()
    for ch in chunks[:-1]:
        reduce_wait(ch)
        attend_bwd(ch)
    for copy in row_copies + col_copies:
        copy.wait()
    high = rloc[...]
    for o in range(1, nt):
        high = jnp.maximum(high, rbuf[o])
    rmax_ref[...] = high
    high = cloc[...]
    for o in range(1, nd):
        high = jnp.maximum(high, cbuf[o])
    cmax_ref[...] = high
    reduce_wait(PARTS - 1)
    attend_bwd(PARTS - 1)

    for ch in chunks:

        @pl.when(has_up)
        def _():
            up(z, ch, True).wait_send()

        @pl.when(has_down)
        def _():
            down(z, ch, True).wait_send()

        spread_done(z, ch, True)
        for dist in range(1, nz):

            @pl.when(z - dist >= 0)
            def _():
                @pl.when(has_up)
                def _():
                    up(z - dist, ch, False).wait_send()

                spread_done(z - dist, ch, False)

            @pl.when(z + dist < nz)
            def _():
                @pl.when(has_down)
                def _():
                    down(z + dist, ch, False).wait_send()

                spread_done(z + dist, ch, False)

        for o in range(1, nd):
            to_partner((d + o) % nd, ch).wait_send()
        for way in range(2):
            att_send(way, ch).wait_send()
            att_relay(way, ch).wait_send()
            first_hop(way, 0, ch).wait_send()
            first_hop(way, 1, ch).wait_send()
            second_hop(way, ch).wait_send()
    for pair in put_out:
        pair[0].wait()
        pair[1].wait()


def fused(queries, keys, values, grad_out, weight, first_code, second_code,
          first_rows, first_cols, second_rows, second_cols, nd, nz):
    length, width = grad_out.shape
    total = weight.shape[0]
    rows = length // PARTS
    heads = width // HD
    nt = CORES * nz
    tile = 256
    tiles = total // tile
    half = jnp.bfloat16
    single = jnp.float32
    dma = pltpu.SemaphoreType.DMA
    vmem = pltpu.VMEM
    inside = pl.BlockSpec(memory_space=pltpu.VMEM)
    outside = pl.BlockSpec(memory_space=pl.ANY)
    blocks = total // HD
    return pl.pallas_call(
        functools.partial(fused_kernel, nd, nz),
        out_shape=(
            jax.ShapeDtypeStruct((length, width), half),
            jax.ShapeDtypeStruct((total, width), half),
            jax.ShapeDtypeStruct((total, width), half),
            jax.ShapeDtypeStruct((2, blocks, HD), single),
            jax.ShapeDtypeStruct((2, width), single),
        ),
        in_specs=[inside] * 4 + [outside] * 3 + [inside] * 4,
        out_specs=(inside, outside, outside, inside, inside),
        scratch_shapes=[
            vmem((nz, PARTS, rows, width), half),
            vmem((PARTS, CORES, nd, rows, width), half),
            vmem((total, nd * length), half),
            vmem((nd, length, width), half),
            vmem((total, width), half),
            vmem((2, tile, width), single),
            vmem((PARTS, nd, rows, width), half),
            vmem((PARTS, 2, rows, width), half),
            vmem((PARTS, rows, width), half),
            vmem((PARTS, rows, width), half),
            vmem((heads, length, length), single),
            vmem((total, width), half),
            vmem((total, width), half),
            vmem((total, HD), single),
            vmem((total, HD), single),
            vmem((2, blocks, HD), single),
            vmem((2, width), single),
            vmem((2, 8, width), single),
            vmem((nt, 2, blocks, HD), single),
            vmem((nd, 2, width), single),
            vmem((length, HD), half),
            vmem((length, HD), half),
            dma((nz, PARTS)),
            dma((nz, PARTS)),
            dma((nz, PARTS)),
            dma((PARTS,)),
            dma((nz, PARTS)),
            dma((nd, PARTS)),
            dma((nd, PARTS)),
            dma((nd, PARTS)),
            dma((2, PARTS)),
            dma((3, nd, PARTS)),
            dma((2, PARTS)),
            dma((2, 2, PARTS)),
            dma((2, 2, PARTS)),
            dma((2, PARTS)),
            dma((2, PARTS)),
            dma((2,)),
            dma((2,)),
            dma((2, tiles)),
            dma((nt,)),
            dma((nt,)),
            dma((nd,)),
            dma((nd,)),
        ],
        compiler_params=pltpu.CompilerParams(
            collective_id=2, has_side_effects=True, vmem_limit_bytes=66 * 1024 * 1024
        ),
    )(
        queries, keys, values, grad_out, weight, first_code, second_code,
        first_rows.reshape(blocks, HD), first_cols.reshape(1, width),
        second_rows.reshape(blocks, HD), second_cols.reshape(1, width),
    )


def finish_kernel(fn_ref, sn_ref, w_ref, rmax_ref, cmax_ref, nw_ref, f_ref, s_ref):
    rows, width = fn_ref.shape
    i = pl.program_id(0)
    count = rows // HD
    for k in range(count):
        at = pl.ds(k * HD, HD)

        def column(m):
            row = 1.0 / (rmax_ref[m, pl.ds(i * count + k, 1)] + code_eps)
            return jnp.broadcast_to(row, (HD, HD)).T

        col1, col2 = column(0), column(1)
        for j in range(width // HD):
            lanes = pl.ds(j * HD, HD)
            first = fn_ref[at, lanes].astype(jnp.float32)
            second = sn_ref[at, lanes].astype(jnp.float32)
            weight = w_ref[at, lanes]
            step = first / correct_first / (jnp.sqrt(second / correct_second) + adam_eps)
            nw_ref[at, lanes] = weight - learning * (step + decay_rate * weight)
            inv1 = 1.0 / (cmax_ref[0:1, lanes] + code_eps)
            inv2 = 1.0 / (cmax_ref[1:2, lanes] + code_eps)
            f_ref[at, lanes] = (first * jnp.maximum(col1, inv1)).astype(jnp.bfloat16)
            s_ref[at, lanes] = (second * jnp.maximum(col2, inv2)).astype(jnp.bfloat16)


def finish(first, second, weight, rmax, cmax):
    total, width = weight.shape
    tile = 256
    big = pl.BlockSpec((tile, width), lambda i: (i, 0))
    whole = lambda x: pl.BlockSpec(x.shape, lambda i: (0,) * x.ndim)
    return pl.pallas_call(
        finish_kernel,
        grid=(total // tile,),
        in_specs=[big, big, big, whole(rmax), whole(cmax)],
        out_specs=(big, big, big),
        out_shape=(
            jax.ShapeDtypeStruct(weight.shape, jnp.float32),
            jax.ShapeDtypeStruct(weight.shape, jnp.bfloat16),
            jax.ShapeDtypeStruct(weight.shape, jnp.bfloat16),
        ),
    )(first, second, weight, rmax, cmax)


def per_device(
    queries,
    keys,
    values,
    grad_out,
    weight,
    first_code,
    first_rows,
    first_cols,
    second_code,
    second_rows,
    second_cols,
):
    dp_count = lax.axis_size("dp")
    cols_dev = queries.shape[1]
    heads_dev = cols_dev // HD
    rows_dev = weight.shape[0]
    width_pad = dp_count * rows_dev
    tensor_count, feats = lax.axis_size("tensor"), grad_out.shape[1]
    if (
        dp_count == 4
        and tensor_count == CORES * dp_count
        and rows_dev == CORES * feats
        and rows_dev % 256 == 0
        and queries.shape[0] == PARTS * HD
    ):
        grad_queries, first, second, rmax, cmax = fused(
            queries, keys, values, grad_out, weight, first_code, second_code,
            first_rows, first_cols, second_rows, second_cols, dp_count, tensor_count // CORES,
        )
        new_weight, first, second = finish(first, second, weight, rmax, cmax)
        return (
            grad_queries,
            new_weight,
            first,
            rmax[0].reshape(rows_dev),
            cmax[0],
            second,
            rmax[1].reshape(rows_dev),
            cmax[1],
        )
    tensor_index = lax.axis_index("tensor")
    kv_start = tensor_index * heads_dev // (H // KVH) * HD
    weight_half = weight.astype(jnp.bfloat16)
    length = queries.shape[0]
    key_sel = lax.dynamic_slice_in_dim(keys, kv_start, HD, 1)
    value_sel = lax.dynamic_slice_in_dim(values, kv_start, HD, 1)
    probabilities, attended = attend(queries, key_sel, value_sel, heads_dev)
    flat = lax.all_gather(grad_out, "tensor", axis=1, tiled=True)
    flat = jnp.pad(flat, ((0, 0), (0, width_pad - flat.shape[1])))
    blocks = jnp.moveaxis(flat.reshape(length, dp_count, 1, rows_dev), 0, 2)
    mine = lax.all_to_all(blocks, "dp", 0, 0, tiled=True)
    all_attended = lax.all_gather(attended, "dp", axis=0, tiled=True)
    mine = mine[:, 0].reshape(dp_count * length, rows_dev)
    partial = jnp.dot(mine, weight_half, preferred_element_type=jnp.float32)
    partial, all_attended = lax.optimization_barrier(
        (partial.astype(jnp.bfloat16), all_attended)
    )
    grad_half = lax.psum_scatter(
        partial, "dp", scatter_dimension=0, tiled=True
    )
    weight_grad = jnp.einsum(
        "sc,sh->ch", mine, all_attended, preferred_element_type=jnp.float32
    )
    grad_queries = attend_back(probabilities, attended, grad_half, key_sel, value_sel, heads_dev)
    first = first_code.astype(jnp.float32) * jnp.minimum(first_rows[:, None], first_cols[None, :])
    second = second_code.astype(jnp.float32) * jnp.minimum(
        second_rows[:, None], second_cols[None, :]
    )
    first_new = beta_first * first + (1.0 - beta_first) * weight_grad
    second_new = beta_second * second + (1.0 - beta_second) * weight_grad * weight_grad
    step_size = first_new / correct_first / (jnp.sqrt(second_new / correct_second) + adam_eps)
    new_weight = weight - learning * (step_size + decay_rate * weight)
    first_abs = jnp.abs(first_new)
    second_abs = jnp.abs(second_new)
    local_rows_max = jnp.stack([jnp.max(first_abs, axis=1), jnp.max(second_abs, axis=1)])
    local_cols_max = jnp.stack([jnp.max(first_abs, axis=0), jnp.max(second_abs, axis=0)])
    rows_mine, cols_mine = maxima(local_rows_max, local_cols_max, dp_count, tensor_count)
    next_first_code = (
        first_new / (jnp.minimum(rows_mine[0][:, None], cols_mine[0][None, :]) + code_eps)
    ).astype(jnp.bfloat16)
    next_second_code = (
        second_new / (jnp.minimum(rows_mine[1][:, None], cols_mine[1][None, :]) + code_eps)
    ).astype(jnp.bfloat16)
    return (
        grad_queries,
        new_weight,
        next_first_code,
        rows_mine[0],
        cols_mine[0],
        next_second_code,
        rows_mine[1],
        cols_mine[1],
    )


def solution(mesh):
    return jax.shard_map(
        per_device,
        mesh=mesh,
        in_specs=(
            P("dp", "tensor"),
            P("dp", None),
            P("dp", None),
            P("dp", "tensor"),
            P("dp", "tensor"),
            P("dp", "tensor"),
            P("dp"),
            P("tensor"),
            P("dp", "tensor"),
            P("dp"),
            P("tensor"),
        ),
        out_specs=(
            P("dp", "tensor"),
            P("dp", "tensor"),
            P("dp", "tensor"),
            P("dp"),
            P("tensor"),
            P("dp", "tensor"),
            P("dp"),
            P("tensor"),
        ),
        check_vma=False,
    )
```

time: 181 us -> 153 us (0.85)
  Pallas kernels: 89.2 us -> 148 us
  other arithmetic: 40.6 us -> 0 us
  matrix products: 24.7 us -> 0 us
  between operations: 14.4 us -> 0.67 us
  local copies, waits for them, and re-layouts: 10.2 us -> 2.1 us
    pallas_call x2, Pallas kernels: 89.2 us -> 148 us  [the longest x1 131 us: fused(): pl.pallas_call(functools.partial(fused_kernel, nd, nz), out_shape=(jax.Sh...]
    convert_element_type x2 -> x0, other arithmetic: 26.8 us -> none  [the longest x1 20.6 us: per_device(): next_second_code = (second_new / (jnp.minimum(rows_mine[1][:, None], cols...]
    dot_general x7 -> x0, matrix products: 24.7 us -> none  [the longest x2 10.1 us: per_device(): jnp.einsum('sc,sh->ch', parts[k], all_attended, preferred_element_type=jn...]
    reduce_max x1 -> x0, other arithmetic: 10.8 us -> none  [per_device(): jnp.max(first_abs, axis=0)]
    slice x3 -> x1, local copies, waits for them, and re-layouts: 5.8 us -> 0.6 us  [per_device(): cmax[1]]
  transfers between devices with their start and end apart: 1 -> 0, of which waited for: 0 -> 0; matrix products, arithmetic and copies ran while one was open for 25% -> 0% of each run, Pallas kernels for 4% -> 0%
where the time goes in v1:
time: 153 us; the launch traced here: 150 us
  Pallas kernels  148 us (97%)
  local copies, waits for them, and re-layouts  2.1 us (1%)
    pallas_call x1, Pallas kernels, fused(): pl.pallas_call(functools.partial(fused_kernel, nd, nz), out_shape=(jax.Sh...  131 us
    pallas_call x1, Pallas kernels, finish(): pl.pallas_call(finish_kernel, grid=(total // tile,), in_specs=[big, big,...  16.7 us

profile of v1, /device:TPU:7, one launch (start us, length us, event | category | flops | bytes accessed | tf_op | source)
XLA Modules:
  0.0 150.4 jit_solution(8841958599681141709)
XLA Ops:
  0.6 131.0 %shard_map.170 = (bf16[384,1024]{1,0:T(8,128)(2,1)}, bf16[2048,1024]{1,0:T(8,128)(2,1)}, bf16[2048,1024]{1,0:T(8,128)(2,1)}, f32[2,16,128]{2,1,0:T(8,128)}, f32[2,1024]{1,0:T(2,128)}) custom-call(bf16[384,1024]{1,0:T(8,128)(2,1)} %q_ref.1, bf16[384,1024]{1,0:T(8,128)(2,1)} %k_ref.1, bf16[384,1024]{1,0:T(8,128)(2,1)} %v_ref.1, bf16[384,1024]{1,0:T(8,128)(2,1)} %grad_ref.1, ...), custom_call_target="tpu_custom_call" | custom-call | tf_op jit(solution)/shard_map/pallas_call | solution.py:642
  131.7 0.0 copy-start.1
  131.7 0.0 copy-start.2
  131.7 0.0 copy-start
  131.7 16.7 %shard_map.171 = (f32[2048,1024]{1,0:T(8,128)}, bf16[2048,1024]{1,0:T(8,128)(2,1)}, bf16[2048,1024]{1,0:T(8,128)(2,1)}) custom-call(bf16[2048,1024]{1,0:T(8,128)(2,1)} %get-tuple-element.17.fn_ref, bf16[2048,1024]{1,0:T(8,128)(2,1)} %get-tuple-element.18.sn_ref, f32[2048,1024]{1,0:T(8,128)} %w_ref.1, f32[2,16,128]{2,1,0:T(8,128)} %get-tuple-element.19.rmax_ref, ...), custom_call_target="tpu_custom_call" | custom-call | tf_op jit(solution)/shard_map/pallas_call | solution.py:739
  148.3 0.0 copy-done.1
  148.3 0.6 slice_bitcast_fusion
  149.0 0.0 copy-done.2
  149.0 0.6 fusion
  149.6 0.0 copy-done
  149.6 0.9 copy.20
Async XLA Ops:
  131.7 16.7 %copy-start.1 = (f32[2,16,128]{2,1,0:T(8,128)S(1)}, f32[2,16,128]{2,1,0:T(8,128)}, u32[]{:S(2)}) copy-start(f32[2,16,128]{2,1,0:T(8,128)} %get-tuple-element.19.rmax_ref) | copy-start | bytes 49156
  131.7 17.3 %copy-start.2 = (f32[2,1024]{1,0:T(2,128)S(1)}, f32[2,1024]{1,0:T(2,128)}, u32[]{:S(2)}) copy-start(f32[2,1024]{1,0:T(2,128)} %get-tuple-element.20.cmax_ref) | copy-start | bytes 24580
  131.7 17.9 %copy-start = (bf16[384,1024]{1,0:T(8,128)(2,1)S(1)}, bf16[384,1024]{1,0:T(8,128)(2,1)}, u32[]{:S(2)}) copy-start(bf16[384,1024]{1,0:T(8,128)(2,1)} %get-tuple-element.36) | copy-start | bytes 2359300

commit v2 on v1

--- a/solution.py
+++ b/solution.py
@@ -121,6 +121,10 @@
 
 
 PARTS = 3
+SPLIT = 2
+SUB = PARTS * SPLIT
+LAG = 2
+TILE = 256
 HALVES = 2
 
 
@@ -131,12 +135,12 @@
 def fused_kernel(
     nd, nz,
     q_ref, k_ref, v_ref, grad_ref, w_hbm, fc_hbm, sc_hbm, fr_ref, fcol_ref, sr_ref, scol_ref,
-    gq_ref, fn_hbm, sn_hbm, rmax_ref, cmax_ref,
-    zbuf, g, gt, a, wh, stage, partial, r1, r2, mid, prob, fcv, scv, rb1, rb2,
+    gq_ref, nw_ref, fcv, scv, rmax_ref, cmax_ref,
+    zbuf, g, gt, a, wh, partial, r1, r2, mid, prob, rb1, rb2, even, odd, racc,
     rloc, cloc, cacc, rbuf, cbuf, kv_k, kv_v,
     up_send, down_send, z_recv, own_send, d_send, d_recv, p_send, p_recv,
     a_send, a_recv, f_send, s1_send, s1_recv, s2_send, s2_recv,
-    w_sem, c_sem, o_sem, rs, rr, cs, cr,
+    w_sem, c_sem, rs, rr, cs, cr,
 ):
     d = lax.axis_index("dp")
     t = lax.axis_index("tensor")
@@ -148,28 +152,31 @@
     dg = 3 - d
     length, width = grad_ref.shape
     rows = length // PARTS
+    fine = length // SUB
     heads = width // HD
     total = w_hbm.shape[0]
     nt = CORES * nz
     has_up = z < nz - 1
     has_down = z > 0
-    tile = stage.shape[1]
+    tile = TILE
     tiles = total // tile
-    far = jnp.abs(z - d)
     alpha, beta = halves(width)
     chunks = range(PARTS)
+    subs = range(SUB)
     scale = HD ** (-0.5)
 
     fetch_w = [
-        pltpu.make_async_copy(w_hbm.at[pl.ds(i * tile, tile)], stage.at[i % 2], w_sem.at[i % 2])
+        pltpu.make_async_copy(
+            w_hbm.at[pl.ds(i * tile, tile)], nw_ref.at[pl.ds(i * tile, tile)], w_sem.at[i]
+        )
         for i in range(tiles)
     ]
     fetch_c = [
         pltpu.make_async_copy(fc_hbm, fcv, c_sem.at[0]),
         pltpu.make_async_copy(sc_hbm, scv, c_sem.at[1]),
     ]
-    fetch_w[0].start()
-    fetch_w[1].start()
+    for copy in fetch_w:
+        copy.start()
 
     barrier = pltpu.get_barrier_semaphore()
     for o in range(1, nt):
@@ -181,8 +188,14 @@
     def part(ch):
         return pl.ds(ch * rows, rows)
 
-    def block(zp, ch, own):
-        return grad_ref.at[part(ch)] if own else zbuf.at[zp, ch]
+    def bit(k):
+        return pl.ds(k * fine, fine)
+
+    def block(zp, k, own):
+        return grad_ref.at[bit(k)] if own else zbuf.at[zp, k]
+
+    def slot(core, src, k):
+        return g.at[k // SPLIT, core, src, bit(k % SPLIT)]
 
     def up(zp, ch, own):
         return pltpu.make_async_remote_copy(
@@ -198,19 +211,19 @@
 
     def to_owner(zp, ch, own):
         return pltpu.make_async_remote_copy(
-            block(zp, ch, own), g.at[ch, c, d], d_send.at[zp, ch], d_recv.at[d, ch],
+            block(zp, ch, own), slot(c, d, ch), d_send.at[zp, ch], d_recv.at[d, ch],
             device_id={"dp": zp},
         )
 
     def keep_partner(zp, ch, own):
         return pltpu.make_async_remote_copy(
-            block(zp, ch, own), g.at[ch, c, d], own_send.at[ch], p_recv.at[d, ch],
+            block(zp, ch, own), slot(c, d, ch), own_send.at[ch], p_recv.at[d, ch],
             device_id={"tensor": partner},
         )
 
     def to_partner(src, ch):
         return pltpu.make_async_remote_copy(
-            g.at[ch, c, src], g.at[ch, c, src], p_send.at[src, ch], p_recv.at[src, ch],
+            slot(c, src, ch), slot(c, src, ch), p_send.at[src, ch], p_recv.at[src, ch],
             device_id={"tensor": partner},
         )
 
@@ -218,7 +231,7 @@
         @pl.when(zp == d)
         def _():
             keep_partner(zp, ch, own).start()
-            g[ch, c, d] = grad_ref[part(ch)] if own else zbuf[zp, ch]
+            g[ch // SPLIT, c, d, bit(ch % SPLIT)] = grad_ref[bit(ch)] if own else zbuf[zp, ch]
 
         @pl.when(zp != d)
         def _():
@@ -237,14 +250,14 @@
         for o in range(1, nd):
             src = (d + o) % nd
             pltpu.make_async_remote_copy(
-                g.at[ch, c, src], g.at[ch, c, src], p_send.at[src, ch], d_recv.at[src, ch],
+                slot(c, src, ch), slot(c, src, ch), p_send.at[src, ch], d_recv.at[src, ch],
                 device_id={"tensor": partner},
             ).wait_recv()
             to_partner(src, ch).start()
 
     def att_send(way, ch):
         return pltpu.make_async_remote_copy(
-            a.at[d, part(ch)], a.at[d, part(ch)], a_send.at[way, ch], a_recv.at[0, d, ch],
+            a.at[d, bit(ch)], a.at[d, bit(ch)], a_send.at[way, ch], a_recv.at[0, d, ch],
             device_id={"dp": (xn, yn)[way]},
         )
 
@@ -252,7 +265,7 @@
         src = (xn, yn)[way]
         half = (alpha, beta)[way]
         return pltpu.make_async_remote_copy(
-            a.at[src, part(ch), half], a.at[src, part(ch), half], f_send.at[way, ch],
+            a.at[src, bit(ch), half], a.at[src, bit(ch), half], f_send.at[way, ch],
             a_recv.at[1 + way, src, ch], device_id={"dp": (yn, xn)[way]},
         )
 
@@ -260,7 +273,7 @@
         for way in range(2):
             src = (xn, yn)[way]
             pltpu.make_async_remote_copy(
-                a.at[src, part(ch)], a.at[src, part(ch)], a_send.at[way, ch],
+                a.at[src, bit(ch)], a.at[src, bit(ch)], a_send.at[way, ch],
                 a_recv.at[0, src, ch], device_id={"dp": src},
             ).wait_recv()
             att_relay(way, ch).start()
@@ -269,7 +282,7 @@
         for way in range(2):
             half = (alpha, beta)[way]
             pltpu.make_async_remote_copy(
-                a.at[dg, part(ch), half], a.at[dg, part(ch), half], f_send.at[way, ch],
+                a.at[dg, bit(ch), half], a.at[dg, bit(ch), half], f_send.at[way, ch],
                 a_recv.at[1 + way, dg, ch], device_id={"dp": (yn, xn)[way]},
             ).wait_recv()
 
@@ -291,9 +304,7 @@
 
     def cast_weight(i):
         fetch_w[i].wait()
-        wh[pl.ds(i * tile, tile)] = stage[i % 2].astype(jnp.bfloat16)
-        if i + 2 < tiles:
-            fetch_w[i + 2].start()
+        wh[pl.ds(i * tile, tile)] = nw_ref[pl.ds(i * tile, tile)].astype(jnp.bfloat16)
 
     def project(ch):
         span = 256
@@ -377,58 +388,86 @@
             rb1[pl.ds(k * HD, HD)] = column(fr_ref[pl.ds(k, 1)] * beta_first)
             rb2[pl.ds(k * HD, HD)] = column(sr_ref[pl.ds(k, 1)] * beta_second)
         cacc[...] = jnp.zeros_like(cacc)
-
-    def moments(i):
-        at = pl.ds(i * tile, tile)
-        span = 256
-
+        racc[...] = jnp.zeros_like(racc)
+
+    tall, span = even.shape
+    across = width // span
+    pieces = (total // tall) * across
+
+    def place(it):
+        return (
+            pl.ds(pl.multiple_of(it // across * tall, tall), tall),
+            pl.multiple_of(it % across * span, span),
+        )
+
+    def gradient(it, out):
+        at, start = place(it)
+        out[...] = jnp.dot(
+            gt[at], a[:, :, pl.ds(start, span)].reshape(nd * length, span),
+            preferred_element_type=jnp.float32,
+        )
+
+    def moments(it, grad):
+        at, start = place(it)
+        for j in range(span // HD):
+            lanes = pl.ds(pl.multiple_of(start + j * HD, HD), HD)
+            dw = grad[:, j * HD : (j + 1) * HD]
+            first = fcv[at, lanes].astype(jnp.float32) * jnp.minimum(
+                rb1[at], fcol_ref[:, lanes] * beta_first
+            ) + (1.0 - beta_first) * dw
+            second = scv[at, lanes].astype(jnp.float32) * jnp.minimum(
+                rb2[at], scol_ref[:, lanes] * beta_second
+            ) + (1.0 - beta_second) * dw * dw
+            fcv[at, lanes] = first.astype(jnp.bfloat16)
+            scv[at, lanes] = second.astype(jnp.bfloat16)
+            for m, value in enumerate((jnp.abs(first), jnp.abs(second))):
+                racc[m, at] = jnp.maximum(racc[m, at], value)
+                cacc[m, :, lanes] = jnp.maximum(
+                    cacc[m, :, lanes], jnp.max(value.reshape(tall // 8, 8, HD), axis=0)
+                )
+
+    def pair(n, carry):
+        gradient(2 * n + 1, odd)
+        moments(2 * n, even)
+        gradient(jnp.minimum(2 * n + 2, pieces - 1), even)
+        moments(2 * n + 1, odd)
+        return carry
+
+    def row_high():
+        for m in range(2):
+            for k in range(total // HD):
+                piece = racc[m, pl.ds(k * HD, HD)].T
+                rloc[m, pl.ds(k, 1)] = jnp.max(piece, axis=0, keepdims=True)
+
+    def weight_step(i):
         def body(n, carry):
-            high1, high2 = carry
-            start = pl.multiple_of(n * span, span)
-            grad = jnp.dot(
-                gt[at], a[:, :, pl.ds(start, span)].reshape(nd * length, span),
-                preferred_element_type=jnp.float32,
-            )
-            for j in range(span // HD):
-                lanes = pl.ds(pl.multiple_of(start + j * HD, HD), HD)
-                dw = grad[:, j * HD : (j + 1) * HD]
-                first = fcv[at, lanes].astype(jnp.float32) * jnp.minimum(
-                    rb1[at], fcol_ref[:, lanes] * beta_first
-                ) + (1.0 - beta_first) * dw
-                second = scv[at, lanes].astype(jnp.float32) * jnp.minimum(
-                    rb2[at], scol_ref[:, lanes] * beta_second
-                ) + (1.0 - beta_second) * dw * dw
-                fcv[at, lanes] = first.astype(jnp.bfloat16)
-                scv[at, lanes] = second.astype(jnp.bfloat16)
-                first, second = jnp.abs(first), jnp.abs(second)
-                high1 = jnp.maximum(high1, first)
-                high2 = jnp.maximum(high2, second)
-                cacc[0, :, lanes] = jnp.maximum(
-                    cacc[0, :, lanes], jnp.max(first.reshape(tile // 8, 8, HD), axis=0)
-                )
-                cacc[1, :, lanes] = jnp.maximum(
-                    cacc[1, :, lanes], jnp.max(second.reshape(tile // 8, 8, HD), axis=0)
-                )
-            return high1, high2
-
-        zero = jnp.zeros((tile, HD), jnp.float32)
-        high = lax.fori_loop(0, width // span, body, (zero, zero))
-        for m in range(2):
-            for k in range(tile // HD):
-                piece = high[m][k * HD : (k + 1) * HD].T
-                rloc[m, pl.ds(i * (tile // HD) + k, 1)] = jnp.max(piece, axis=0, keepdims=True)
-
-    put_out = [
-        [
-            pltpu.make_async_copy(
-                fcv.at[pl.ds(i * tile, tile)], fn_hbm.at[pl.ds(i * tile, tile)], o_sem.at[0, i]
-            ),
-            pltpu.make_async_copy(
-                scv.at[pl.ds(i * tile, tile)], sn_hbm.at[pl.ds(i * tile, tile)], o_sem.at[1, i]
-            ),
-        ]
-        for i in range(tiles)
-    ]
+            at = pl.ds(pl.multiple_of(i * tile + n * 32, 32), 32)
+            first = fcv[at].astype(jnp.float32)
+            second = scv[at].astype(jnp.float32)
+            root = jnp.sqrt(second * (1.0 / correct_second)) + adam_eps
+            nw_ref[at] = (1.0 - learning * decay_rate) * nw_ref[at] - (
+                learning / correct_first
+            ) * first / root
+            return carry
+
+        lax.fori_loop(0, tile // 32, body, 0)
+
+    def codes(i):
+        def body(n, carry):
+            k = i * (tile // HD) + n
+            at = pl.ds(pl.multiple_of(k * HD, HD), HD)
+            col1 = column(1.0 / (rmax_ref[0, pl.ds(k, 1)] + code_eps))
+            col2 = column(1.0 / (rmax_ref[1, pl.ds(k, 1)] + code_eps))
+            for j in range(width // HD):
+                lanes = pl.ds(j * HD, HD)
+                inv1 = jnp.maximum(col1, cloc[0:1, lanes])
+                inv2 = jnp.maximum(col2, cloc[1:2, lanes])
+                fcv[at, lanes] = (fcv[at, lanes].astype(jnp.float32) * inv1).astype(jnp.bfloat16)
+                scv[at, lanes] = (scv[at, lanes].astype(jnp.float32) * inv2).astype(jnp.bfloat16)
+            return carry
+
+        lax.fori_loop(0, tile // HD, body, 0)
+
     row_copies = [
         pltpu.make_async_remote_copy(
             rloc, rbuf.at[o], rs.at[o], rr.at[o], device_id={"tensor": (t + o) % nt}
@@ -465,106 +504,114 @@
             first_hop(way, 0, ch).wait_recv()
             second_hop(way, ch).wait_recv()
 
-    for ch in chunks:
-
+    def send_own(k):
         @pl.when(has_up)
         def _():
-            up(z, ch, True).start()
+            up(z, k, True).start()
 
         @pl.when(has_down)
         def _():
-            down(z, ch, True).start()
-
-        spread(z, ch, True)
-
+            down(z, k, True).start()
+
+        spread(z, k, True)
+
+    def forward(dist, k):
+        @pl.when(z - dist >= 0)
+        def _():
+            zp = z - dist
+            down(zp, k, False).wait_recv()
+
+            @pl.when(has_up)
+            def _():
+                up(zp, k, False).start()
+
+            spread(zp, k, False)
+
+        @pl.when(z + dist < nz)
+        def _():
+            zp = z + dist
+            down(zp, k, False).wait_recv()
+
+            @pl.when(has_down)
+            def _():
+                down(zp, k, False).start()
+
+            spread(zp, k, False)
+
+    def gathered(ch):
+        for k in range(ch * SPLIT, (ch + 1) * SPLIT):
+            for src in range(nd):
+                pltpu.make_async_remote_copy(
+                    slot(1 - c, src, k), slot(1 - c, src, k), p_send.at[src, k],
+                    p_recv.at[src, k], device_id={"tensor": partner},
+                ).wait_recv()
+
+    def att_start(k):
+        att_send(0, k).start()
+        att_send(1, k).start()
+
+    send_own(0)
+    send_own(1)
     fetch_c[0].start()
     fetch_c[1].start()
     attend_fwd()
     cast_weight(0)
-    cast_weight(1)
-
     jobs = {
-        0: [lambda: cast_weight(2), lambda: cast_weight(3)],
-        1: [lambda: cast_weight(4), lambda: cast_weight(5)],
-        2: [lambda: cast_weight(6), lambda: cast_weight(7)],
-        3: [scales],
+        (0, 1): [lambda: att_start(0), lambda: att_start(1), lambda: cast_weight(1)],
+        (0, 2): [lambda: cast_weight(2)],
+        (0, 3): [lambda: cast_weight(3)],
+        (1, 1): [lambda: att_start(2), lambda: att_start(3), lambda: cast_weight(4)],
+        (1, 2): [lambda: cast_weight(5)],
+        (1, 3): [lambda: cast_weight(6)],
+        (2, 1): [lambda: att_start(4), lambda: att_start(5), lambda: cast_weight(7)],
+        (2, 2): [scales],
+        (3, 3): [lambda: att_pass(0), lambda: att_pass(1), lambda: att_pass(2)],
+        (4, 1): [lambda: gathered(0), lambda: project(0)],
+        (4, 2): [lambda: turn(0)],
+        (4, 3): [lambda: att_pass(3), lambda: att_pass(4), lambda: att_pass(5),
+                 lambda: reduce_first(0)],
+        (5, 2): [lambda: gathered(1), lambda: project(1)],
     }
-    step = 0
-    for dist in range(1, nz):
-        for ch in chunks:
-
-            @pl.when(z - dist >= 0)
-            def _():
-                zp = z - dist
-                down(zp, ch, False).wait_recv()
-
-                @pl.when(has_up)
-                def _():
-                    up(zp, ch, False).start()
-
-                spread(zp, ch, False)
-
-            @pl.when(z + dist < nz)
-            def _():
-                zp = z + dist
-                down(zp, ch, False).wait_recv()
-
-                @pl.when(has_down)
-                def _():
-                    down(zp, ch, False).start()
-
-                spread(zp, ch, False)
-
-            if dist == 1:
-                att_send(0, ch).start()
-                att_send(1, ch).start()
-
-            @pl.when(far == dist - 1)
-            def _():
-                pass_on(ch)
-
-            if dist == 3:
-                att_pass(ch)
-            for job in jobs.get(step, []):
+    for k in subs:
+        if k >= LAG:
+            pass_on(k - LAG)
+        for dist in range(1, nz):
+            forward(dist, k)
+            if dist == 1 and k + 2 < SUB:
+                send_own(k + 2)
+            for job in jobs.get((k, dist), []):
                 job()
-            step += 1
-    last = nz - 1
-
-    def gathered(ch):
-        @pl.when(far == last)
-        def _():
-            pass_on(ch)
-
-        for src in range(nd):
-            pltpu.make_async_remote_copy(
-                g.at[ch, 1 - c, src], g.at[ch, 1 - c, src], p_send.at[src, ch],
-                p_recv.at[src, ch], device_id={"tensor": partner},
-            ).wait_recv()
-
-    for ch in chunks:
-        gathered(ch)
-        project(ch)
-        turn(ch)
-        reduce_first(ch)
+    reduce_first(1)
+    pass_on(SUB - 2)
+    pass_on(SUB - 1)
+    turn(1)
+    gathered(2)
+    project(2)
+    reduce_first(2)
+    reduce_mid(0)
+    turn(2)
+    reduce_next(0)
     for copy in fetch_c:
         copy.wait()
-    for ch in chunks:
+    for ch in subs:
         att_wait(ch)
-    after = {2: lambda: reduce_mid(0), 3: lambda: reduce_next(0), 4: lambda: reduce_mid(1),
-             5: lambda: reduce_next(1), 6: lambda: reduce_mid(2), 7: lambda: reduce_next(2)}
-    for i in range(tiles):
-        moments(i)
-        if i in after:
-            after[i]()
-        if i:
-            put_out[i - 1][0].start()
-            put_out[i - 1][1].start()
+    gradient(0, even)
+    reduce_mid(1)
+    lax.fori_loop(0, 1, pair, 0)
+    reduce_next(1)
+    lax.fori_loop(1, pieces // 4, pair, 0)
+    reduce_mid(2)
+    lax.fori_loop(pieces // 4, pieces // 4 + 1, pair, 0)
+    reduce_next(2)
+    lax.fori_loop(pieces // 4 + 1, pieces // 2, pair, 0)
+    row_high()
     for m in range(2):
         cloc[pl.ds(m, 1)] = jnp.max(cacc[m], axis=0, keepdims=True)
-    put_out[tiles - 1][0].start()
-    put_out[tiles - 1][1].start()
+    weight_step(0)
     for copy in row_copies + col_copies:
         copy.start()
+    for i in range(1, tiles):
+        weight_step(i)
     for ch in chunks[:-1]:
         reduce_wait(ch)
         attend_bwd(ch)
@@ -578,10 +625,13 @@
     for o in range(1, nd):
         high = jnp.maximum(high, cbuf[o])
     cmax_ref[...] = high
-    reduce_wait(PARTS - 1)
-    attend_bwd(PARTS - 1)
-
-    for ch in chunks:
+    cloc[...] = 1.0 / (high + code_eps)
+    for i in range(tiles):
+        codes(i)
+    reduce_wait(2)
+    attend_bwd(2)
+
+    for ch in subs:
 
         @pl.when(has_up)
         def _():
@@ -615,12 +665,11 @@
         for way in range(2):
             att_send(way, ch).wait_send()
             att_relay(way, ch).wait_send()
+    for ch in chunks:
+        for way in range(2):
             first_hop(way, 0, ch).wait_send()
             first_hop(way, 1, ch).wait_send()
             second_hop(way, ch).wait_send()
-    for pair in put_out:
-        pair[0].wait()
-        pair[1].wait()
 
 
 def fused(queries, keys, values, grad_out, weight, first_code, second_code,
@@ -630,8 +679,7 @@
     rows = length // PARTS
     heads = width // HD
     nt = CORES * nz
-    tile = 256
-    tiles = total // tile
+    tiles = total // TILE
     half = jnp.bfloat16
     single = jnp.float32
     dma = pltpu.SemaphoreType.DMA
@@ -642,30 +690,31 @@
     return pl.pallas_call(
         functools.partial(fused_kernel, nd, nz),
         out_shape=(
-            jax.ShapeDtypeStruct((length, width), half),
-            jax.ShapeDtypeStruct((total, width), half),
-            jax.ShapeDtypeStruct((total, width), half),
-            jax.ShapeDtypeStruct((2, blocks, HD), single),
-            jax.ShapeDtypeStruct((2, width), single),
+            vmem((length, width), half),
+            vmem((total, width), single),
+            vmem((total, width), half),
+            vmem((total, width), half),
+            vmem((2, blocks, HD), single),
+            vmem((2, width), single),
         ),
         in_specs=[inside] * 4 + [outside] * 3 + [inside] * 4,
-        out_specs=(inside, outside, outside, inside, inside),
+        out_specs=(inside,) * 6,
         scratch_shapes=[
-            vmem((nz, PARTS, rows, width), half),
+            vmem((nz, SUB, length // SUB, width), half),
             vmem((PARTS, CORES, nd, rows, width), half),
             vmem((total, nd * length), half),
             vmem((nd, length, width), half),
             vmem((total, width), half),
-            vmem((2, tile, width), single),
             vmem((PARTS, nd, rows, width), half),
             vmem((PARTS, 2, rows, width), half),
             vmem((PARTS, rows, width), half),
             vmem((PARTS, rows, width), half),
             vmem((heads, length, length), single),
-            vmem((total, width), half),
-            vmem((total, width), half),
             vmem((total, HD), single),
             vmem((total, HD), single),
+            vmem((512, 256), single),
+            vmem((512, 256), single),
+            vmem((2, total, HD), single),
             vmem((2, blocks, HD), single),
             vmem((2, width), single),
             vmem((2, 8, width), single),
@@ -673,80 +722,36 @@
             vmem((nd, 2, width), single),
             vmem((length, HD), half),
             vmem((length, HD), half),
-            dma((nz, PARTS)),
-            dma((nz, PARTS)),
-            dma((nz, PARTS)),
-            dma((PARTS,)),
-            dma((nz, PARTS)),
-            dma((nd, PARTS)),
-            dma((nd, PARTS)),
-            dma((nd, PARTS)),
-            dma((2, PARTS)),
-            dma((3, nd, PARTS)),
-            dma((2, PARTS)),
+            dma((nz, SUB)),
+            dma((nz, SUB)),
+            dma((nz, SUB)),
+            dma((SUB,)),
+            dma((nz, SUB)),
+            dma((nd, SUB)),
+            dma((nd, SUB)),
+            dma((nd, SUB)),
+            dma((2, SUB)),
+            dma((3, nd, SUB)),
+            dma((2, SUB)),
             dma((2, 2, PARTS)),
             dma((2, 2, PARTS)),
             dma((2, PARTS)),
             dma((2, PARTS)),
+            dma((tiles,)),
             dma((2,)),
-            dma((2,)),
-            dma((2, tiles)),
             dma((nt,)),
             dma((nt,)),
             dma((nd,)),
             dma((nd,)),
         ],
         compiler_params=pltpu.CompilerParams(
-            collective_id=2, has_side_effects=True, vmem_limit_bytes=66 * 1024 * 1024
+            collective_id=2, has_side_effects=True, vmem_limit_bytes=46 * 1024 * 1024
         ),
     )(
         queries, keys, values, grad_out, weight, first_code, second_code,
         first_rows.reshape(blocks, HD), first_cols.reshape(1, width),
         second_rows.reshape(blocks, HD), second_cols.reshape(1, width),
     )
-
-
-def finish_kernel(fn_ref, sn_ref, w_ref, rmax_ref, cmax_ref, nw_ref, f_ref, s_ref):
-    rows, width = fn_ref.shape
-    i = pl.program_id(0)
-    count = rows // HD
-    for k in range(count):
-        at = pl.ds(k * HD, HD)
-
-        def column(m):
-            row = 1.0 / (rmax_ref[m, pl.ds(i * count + k, 1)] + code_eps)
-            return jnp.broadcast_to(row, (HD, HD)).T
-
-        col1, col2 = column(0), column(1)
-        for j in range(width // HD):
-            lanes = pl.ds(j * HD, HD)
-            first = fn_ref[at, lanes].astype(jnp.float32)
-            second = sn_ref[at, lanes].astype(jnp.float32)
-            weight = w_ref[at, lanes]
-            step = first / correct_first / (jnp.sqrt(second / correct_second) + adam_eps)
-            nw_ref[at, lanes] = weight - learning * (step + decay_rate * weight)
-            inv1 = 1.0 / (cmax_ref[0:1, lanes] + code_eps)
-            inv2 = 1.0 / (cmax_ref[1:2, lanes] + code_eps)
-            f_ref[at, lanes] = (first * jnp.maximum(col1, inv1)).astype(jnp.bfloat16)
-            s_ref[at, lanes] = (second * jnp.maximum(col2, inv2)).astype(jnp.bfloat16)
-
-
-def finish(first, second, weight, rmax, cmax):
-    total, width = weight.shape
-    tile = 256
-    big = pl.BlockSpec((tile, width), lambda i: (i, 0))
-    whole = lambda x: pl.BlockSpec(x.shape, lambda i: (0,) * x.ndim)
-    return pl.pallas_call(
-        finish_kernel,
-        grid=(total // tile,),
-        in_specs=[big, big, big, whole(rmax), whole(cmax)],
-        out_specs=(big, big, big),
-        out_shape=(
-            jax.ShapeDtypeStruct(weight.shape, jnp.float32),
-            jax.ShapeDtypeStruct(weight.shape, jnp.bfloat16),
-            jax.ShapeDtypeStruct(weight.shape, jnp.bfloat16),
-        ),
-    )(first, second, weight, rmax, cmax)
 
 
 def per_device(
@@ -772,14 +777,13 @@
         dp_count == 4
         and tensor_count == CORES * dp_count
         and rows_dev == CORES * feats
-        and rows_dev % 256 == 0
+        and rows_dev % 1024 == 0
         and queries.shape[0] == PARTS * HD
     ):
-        grad_queries, first, second, rmax, cmax = fused(
+        grad_queries, new_weight, first, second, rmax, cmax = fused(
             queries, keys, values, grad_out, weight, first_code, second_code,
             first_rows, first_cols, second_rows, second_cols, dp_count, tensor_count // CORES,
         )
-        new_weight, first, second = finish(first, second, weight, rmax, cmax)
         return (
             grad_queries,
             new_weight,

time: 153 us -> 134 us (0.88); the launches traced: 150 us -> 134 us
  Pallas kernels: 148 us -> 124 us
  local copies, waits for them, and re-layouts: 2.1 us -> 9.51 us
    pallas_call x2 -> x1, Pallas kernels: 148 us -> 124 us  [fused(): pl.pallas_call(functools.partial(fused_kernel, nd, nz), out_shape=(vmem((...]
    unnamed x7 -> x4, local copies, waits for them, and re-layouts: 0.89 us -> 8.3 us
where the time goes in v2:
time: 134 us
  Pallas kernels  124 us (93%)
  local copies, waits for them, and re-layouts  9.51 us (7%)
    pallas_call x1, Pallas kernels, fused(): pl.pallas_call(functools.partial(fused_kernel, nd, nz), out_shape=(vmem((...  124 us
    unnamed x4, local copies, waits for them, and re-layouts  8.3 us

profile of v2, /device:TPU:7, one launch (start us, length us, event | category | flops | bytes accessed | tf_op | source)
XLA Modules:
  0.0 133.7 jit_solution(542698549451660534)
XLA Ops:
  0.6 123.6 %shard_map.170 = (bf16[384,1024]{1,0:T(8,128)(2,1)S(1)}, f32[2048,1024]{1,0:T(8,128)S(1)}, bf16[2048,1024]{1,0:T(8,128)(2,1)S(1)}, bf16[2048,1024]{1,0:T(8,128)(...) custom-call(bf16[384,1024]{1,0:T(8,128)(2,1)} %q_ref.1, bf16[384,1024]{1,0:T(8,128)(2,1)} %k_ref.1, ...), custom_call_target="tpu_custom_call" | custom-call | tf_op jit(solution)/shard_map/pallas_call | solution.py:690
  124.2 0.9 copy.23
  125.1 0.6 fusion
  125.7 0.6 slice_bitcast_fusion
  126.3 2.0 %copy.25 = bf16[2048,1024]{1,0:T(8,128)(2,1)} copy(bf16[2048,1024]{1,0:T(8,128)(2,1)S(1)} %get-tuple-element.26) | data formatting | bytes 8388608
  128.3 2.0 %copy.26 = bf16[2048,1024]{1,0:T(8,128)(2,1)} copy(bf16[2048,1024]{1,0:T(8,128)(2,1)S(1)} %get-tuple-element.29) | data formatting | bytes 8388608
  130.3 3.4 %copy.24 = f32[2048,1024]{1,0:T(8,128)} copy(f32[2048,1024]{1,0:T(8,128)S(1)} %get-tuple-element.25) | data formatting | bytes 16777216
